TPU v7x, 32 devices: a whole 2x2x4 slice. The times are simulated.
32 devices in a mesh: data: 32 (over z, y, x, core).
Axes of the slice: x: 2, y: 2, z: 4, core: 2. Of those that a mesh axis runs over, the one named last changes fastest.
Arguments:
- act_in: bfloat16 [16384, 1024], P('data')
- pre_act: bfloat16 [16384, 4096], P('data')
- grad_out: bfloat16 [16384, 4096], P('data')
- q_init: float32 [4096, 8], replicated
- err_mem: float32 [32, 1024, 4096], P('data')
Outputs:
- output 1: float32 [1024, 8], replicated
- output 2: float32 [4096, 8], replicated
- output 3: float32 [32, 1024, 4096], P('data')
All inputs are finite; a program needn't handle non-finite values.
Results may differ from a plain program's by a relative error of at most 0.001.
Values sent between devices are 32-bit elements.
A program may use at most 1 GiB of HBM per device.

v0:
```python
import jax
import jax.numpy as jnp
from jax import lax
from jax.sharding import PartitionSpec as P

EXACT_PREC = lax.Precision.HIGHEST


def gelu_grad(pre_act, grad_out):
    z_f32 = pre_act.astype(jnp.float32)
    _, pullback = jax.vjp(jax.nn.gelu, z_f32)
    return pullback(grad_out.astype(jnp.float32))[0]


def orthonormalize(p_sum):
    def gs_step(col_idx, ortho_cols):
        column = lax.dynamic_slice_in_dim(p_sum, col_idx, 1, axis=1)
        proj_coef = jnp.dot(column.T, ortho_cols, precision=EXACT_PREC)
        residual = column - jnp.dot(ortho_cols, proj_coef.T, precision=EXACT_PREC)
        unit_col = residual / jnp.sqrt(jnp.sum(residual * residual))
        return lax.dynamic_update_slice_in_dim(ortho_cols, unit_col, col_idx, axis=1)
    return lax.fori_loop(0, p_sum.shape[1], gs_step, jnp.zeros_like(p_sum))


def solution(mesh):
    group_size = mesh.shape['data']

    def per_device(act_in, pre_act, grad_out, q_init, err_mem):
        row_count = act_in.shape[0]
        grad_pre = gelu_grad(pre_act, grad_out).astype(jnp.bfloat16)
        grad_w = lax.dot_general(act_in, grad_pre, (((0,), (0,)), ((), ())), preferred_element_type=jnp.float32)
        merged = grad_w / row_count + err_mem[0]
        p_part = jnp.dot(merged, q_init, precision=EXACT_PREC)
        p_sum = lax.psum(p_part, 'data')
        p_factor = orthonormalize(p_sum)
        q_part = lax.dot_general(merged, p_factor, (((0,), (0,)), ((), ())), precision=EXACT_PREC)
        q_factor = lax.psum(q_part, 'data') / group_size
        approx = lax.dot_general(p_factor, q_factor, (((1,), (1,)), ((), ())), precision=EXACT_PREC)
        err_new = merged - approx
        return p_factor, q_factor, err_new[None]

    return jax.shard_map(per_device, mesh=mesh, in_specs=(P('data', None), P('data', None), P('data', None), P(None, None), P('data', None, None)), out_specs=(P(None, None), P(None, None), P('data', None, None)), check_vma=False)
```

profile of v0, /device:TPU:0, one launch (start us, length us, event | category | flops | bytes accessed | tf_op | source)
XLA Modules:
  0.0 301.3 jit_solution(8130417221267289930)
XLA Ops:
  7.2 0.0 copy-start
  7.2 0.0 all-reduce.2.cloned.1.call-start
  7.2 17.5 %copy.8 = f32[1,1024,4096]{1,2,0:T(8,128)} copy(f32[1,1024,4096]{2,1,0:T(8,128)} %param.11) | data formatting | bytes 33554432 | tf_op args[4]
  24.7 0.0 copy-done
  24.8 0.0 copy-start.4
  24.8 18.2 %bitcast_add_fusion = f32[1024,4096]{0,1:T(8,128)} fusion(f32[1,1024,4096]{1,2,0:T(8,128)} %copy.8, bf16[512,1024]{1,0:T(8,128)(2,1)S(1)} %copy-done, bf16[512,4096]{1,0:T(8,128)(2,1)} %param.9, bf16[512,4096]{1,0:T(8,128)(2,1)} %param.8), kind=kOutput, calls=%fused_computation.7 | convolution fusion | flops 4349493248 | bytes 42991616 | tf_op jit(solution)/shard_map/dot_general | solution.py:31
  42.9 0.0 copy-done.4
  42.9 12.3 %fusion.26 = f32[1024,8]{0,1:T(8,128)S(1)} fusion(f32[1024,4096]{0,1:T(8,128)} %bitcast_add_fusion, f32[4096,8]{0,1:T(8,128)S(1)} %copy-done.4), kind=kOutput, calls=%fused_computation.37 | convolution fusion | flops 402653184 | bytes 16941056 | tf_op jit(solution)/shard_map/dot_general | solution.py:33
  55.2 42.2 %psum.14 = f32[1024,8]{0,1:T(8,128)S(1)} all-reduce(f32[1024,8]{0,1:T(8,128)S(1)} %fusion.26), channel_id=1, replica_groups=mesh['data'=32] {'data'}, use_global_device_ids=true, to_apply=%region_0.0 | all-reduce | flops 8192 | bytes 65536 | tf_op jit(solution)/shard_map/psum | solution.py:34
  97.5 14.4 %while.13 = (s32[]{:T(128)}, f32[1024,8]{0,1:T(8,128)S(1)}, f32[1024,8]{0,1:T(8,128)S(1)}, s32[]{:T(128)}, s32[]{:T(128)}) while((s32[]{:T(128)}, f32[1024,8]{0,1:T(8,128)S(1)}, f32[1024,8]{0,1:T(8,128)S(1)}, s32[]{:T(128)}, s32[]{:T(128)}) %tuple.36), condition=%wide.region_3.0_spmd, body=%wide.region_1.0_spmd.sunk | while | flops 200705 | bytes 94369 | solution.py:22
  97.5 0.2 convolution_bitcast_fusion.3
  97.6 0.8 multiply_reduce_fusion.2
  99.1 0.1 dynamic_update_slice.8
  99.3 0.2 convolution_bitcast_fusion.3
  99.4 0.8 multiply_reduce_fusion.2
  100.9 0.1 dynamic_update_slice.8
  101.1 0.2 convolution_bitcast_fusion.3
  101.2 0.8 multiply_reduce_fusion.2
  102.7 0.1 dynamic_update_slice.8
  102.9 0.2 convolution_bitcast_fusion.3
  103.0 0.8 multiply_reduce_fusion.2
  104.5 0.1 dynamic_update_slice.8
  104.7 0.2 convolution_bitcast_fusion.3
  104.8 0.8 multiply_reduce_fusion.2
  106.3 0.1 dynamic_update_slice.8
  106.5 0.2 convolution_bitcast_fusion.3
  106.6 0.8 multiply_reduce_fusion.2
  108.1 0.1 dynamic_update_slice.8
  108.2 0.2 convolution_bitcast_fusion.3
  108.4 0.8 multiply_reduce_fusion.2
  109.9 0.1 dynamic_update_slice.8
  110.0 0.2 convolution_bitcast_fusion.3
  110.2 0.8 multiply_reduce_fusion.2
  111.7 0.1 dynamic_update_slice.8
  111.8 0.0 copy-start.2
  111.8 18.2 %fusion.27 = f32[4096,8]{0,1:T(8,128)} fusion(f32[1024,4096]{0,1:T(8,128)} %bitcast_add_fusion, f32[1024,8]{0,1:T(8,128)S(1)} %get-tuple-element.68), kind=kOutput, calls=%fused_computation.38 | convolution fusion | flops 402653184 | bytes 16941056 | tf_op jit(solution)/shard_map/dot_general | solution.py:36
  130.0 0.0 all-reduce.2.cloned.1.call-update
  130.0 127.5 %all-reduce.2.cloned.1.call-done = f32[4096,8]{0,1:T(8,128)} async-done(((f32[4096,8]{0,1:T(8,128)}), f32[4096,8]{0,1:T(8,128)}) %all-reduce.2.cloned.1.call-update) | async-done | bytes 131088 | tf_op jit(solution)/shard_map/psum | solution.py:37
  257.5 0.9 broadcast_multiply_fusion
  258.4 0.0 copy-done.2
  258.5 0.0 copy-start.3
  258.5 18.4 %subtract_bitcast_fusion = f32[1,1024,4096]{1,2,0:T(8,128)} fusion(f32[1024,4096]{0,1:T(8,128)} %bitcast_add_fusion, f32[1024,8]{0,1:T(8,128)S(1)} %get-tuple-element.68, f32[4096,8]{0,1:T(8,128)S(1)} %broadcast_multiply_fusion), kind=kOutput, calls=%fused_computation.8 | convolution fusion | flops 406847488 | bytes 33718272 | tf_op jit(solution)/shard_map/dot_general | solution.py:38
  276.9 0.0 copy-done.3
  276.9 0.0 copy-start.1
  276.9 17.5 %copy.10 = f32[1,1024,4096]{2,1,0:T(8,128)} copy(f32[1,1024,4096]{1,2,0:T(8,128)} %subtract_bitcast_fusion) | data formatting | bytes 33554432
  294.4 0.0 copy-done.1
  (9 shorter events, 0.1 us)
Async XLA Ops:
  7.2 17.6 %copy-start = (bf16[512,1024]{1,0:T(8,128)(2,1)S(1)}, bf16[512,1024]{1,0:T(8,128)(2,1)}, u32[]{:S(2)}) copy-start(bf16[512,1024]{1,0:T(8,128)(2,1)} %param.7) | copy-start | bytes 3145732
  7.2 250.3 %all-reduce.2.cloned.1.call-start = ((), (), s32[]{:S(2)}) async-start(), calls=%async_computation | async-start | bytes 262144 | tf_op jit(solution)/shard_map/psum | solution.py:37
  24.8 18.2 %copy-start.4 = (f32[4096,8]{0,1:T(8,128)S(1)}, f32[4096,8]{0,1:T(8,128)}, u32[]{:S(2)}) copy-start(f32[4096,8]{0,1:T(8,128)} %param.10) | copy-start | bytes 393220
  111.8 146.6 %copy-start.2 = (f32[1024,8]{0,1:T(8,128)}, f32[1024,8]{0,1:T(8,128)S(1)}, u32[]{:S(2)}) copy-start(f32[1024,8]{0,1:T(8,128)S(1)} %get-tuple-element.68) | copy-start | bytes 98308
  258.5 18.4 %copy-start.3 = (f32[4096,8]{0,1:T(8,128)}, f32[4096,8]{0,1:T(8,128)S(1)}, u32[]{:S(2)}) copy-start(f32[4096,8]{0,1:T(8,128)S(1)} %broadcast_multiply_fusion) | copy-start | bytes 393220
  276.9 17.5 %copy-start.1 = (bf16[512,1024]{1,0:T(8,128)(2,1)S(1)}, bf16[512,1024]{1,0:T(8,128)(2,1)}, u32[]{:S(2)}) copy-start(bf16[512,1024]{1,0:T(8,128)(2,1)} %param.7) | copy-start | bytes 3145732
Sparse Core Ops, SparseCore 0:
  130.2 127.3 all-reduce.1
where the time goes:
time: 302 us; the launch traced here: 301 us
  waiting for transfers between devices  128 us (42%)
  matrix products  74.7 us (25%)
  blocking collectives  42.2 us (14%)
  local copies, waits for them, and re-layouts  36 us (12%)
  between operations  14.1 us (5%)
  loops' own time  5.79 us (2%)
    psum x1, waiting for transfers between devices, per_device(): q_factor = lax.psum(q_part, 'data') / group_size  127 us
    psum x1, blocking collectives, per_device(): p_sum = lax.psum(p_part, 'data')  42.2 us
    unnamed x12, local copies, waits for them, and re-layouts  35.1 us
    dot_general x1, matrix products, per_device(): lax.dot_general(p_factor, q_factor, (((1,), (1,)), ((), ())), precision=E...  18.4 us
    dot_general x1, matrix products, per_device(): lax.dot_general(act_in, grad_pre, (((0,), (0,)), ((), ())), preferred_ele...  18.2 us
    dot_general x1, matrix products, per_device(): lax.dot_general(merged, p_factor, (((0,), (0,)), ((), ())), precision=EXA...  18.2 us
    dot_general x1, matrix products, per_device(): p_part = jnp.dot(merged, q_init, precision=EXACT_PREC)  12.3 us
    dot_general x8, matrix products, gs_step(): residual = column - jnp.dot(ortho_cols, proj_coef.T, precision=EXACT_PREC)  6.36 us
  transfers between devices with their start and end apart: 1, of which 1 were waited for; matrix products, arithmetic and copies ran while one was open for 0% of the time, Pallas kernels for 0%

commit v1 on v0

v1 whole, which is shorter than its diff:
```python
import functools

import jax
import jax.numpy as jnp
from jax import lax
from jax.experimental import pallas as pl
from jax.experimental.pallas import tpu as pltpu
from jax.sharding import PartitionSpec as P

F32 = jnp.float32
BF16 = jnp.bfloat16
MESH = pl.DeviceIdType.MESH
RANK = 8
CB = 256
RB = 256
NT = (((1,), (1,)), ((), ()))


def split3(x):
    hi = x.astype(BF16)
    rest = x - hi.astype(F32)
    mid = rest.astype(BF16)
    low = (rest - mid.astype(F32)).astype(BF16)
    return hi, mid, low


def stack3(x):
    parts = [p.astype(F32) for p in split3(x)]
    return jnp.concatenate(parts + [jnp.zeros_like(x)], axis=0).astype(BF16)


def fold3(y):
    return (y[16:24] + y[8:16]) + y[0:8]


def mm(a, b):
    return jnp.dot(a, b, preferred_element_type=F32)


def mm_nt(a, b):
    return lax.dot_general(a, b, NT, preferred_element_type=F32)


def gelu_grad(z, dy):
    c = 0.7978845608028654
    x = z.astype(F32)
    x2 = x * x
    t = jnp.tanh(x * (x2 * (c * 0.044715) + c))
    up = 1.0 + t
    slope = ((x * up) * (1.0 - t)) * (x2 * (1.5 * c * 0.044715) + 0.5 * c)
    return (0.5 * up + slope) * dy.astype(F32)


def orthonormalize(p):
    row = lax.broadcasted_iota(jnp.int32, (RANK, 1), 0)
    w = p
    norm2 = jnp.zeros((RANK, 1), F32)
    for j in range(RANK):
        v = w[j:j + 1]
        d = jnp.sum(jnp.where(row > j, p, w) * v, axis=1, keepdims=True)
        norm2 = jnp.where(row == j, d, norm2)
        if j + 1 < RANK:
            coef = jnp.where(row > j, d / d[j:j + 1], 0.0)
            w = w - coef * v
    return w / jnp.sqrt(norm2)


def reduce_kernel(n, a_hbm, z_hbm, dy_hbm, qt_ref, e_hbm, pleft_ref, pt_ref, q_ref, m_ref,
                  parts, g, a_v, at_v, qs, p_acc, h_acc, p_own, p_recv, p_all, y_own, y_recv,
                  in_sem, a_sem, ps_sem, pr_sem, pbs_sem, pbr_sem, ys_sem, yr_sem, ybs_sem, ybr_sem):
    me = lax.axis_index("data")
    d_in, d_out = m_ref.shape
    tokens = g.shape[0]
    nc = d_out // CB
    n_p = d_in // 128
    n_y = n // 2
    cw = d_out // n_y
    base = n // 4
    rel = lax.rem(me + (n - base), n)
    p_owner = (rel < 2 * n_p) & (lax.rem(rel, 2) == 1)
    p_mine = jnp.minimum(lax.div(rel, 2), n_p - 1)
    y_owner = rel < n_y
    y_mine = jnp.minimum(rel, n_y - 1)

    barrier = pltpu.get_barrier_semaphore()

    @pl.loop(1, n)
    def _(k):
        pl.semaphore_signal(barrier, inc=1, device_id=(lax.rem(me + k, n),), device_id_type=MESH)

    def e_copy(c):
        cols = pl.ds(pl.multiple_of(c * CB, CB), CB)
        return pltpu.make_async_copy(e_hbm.at[0, :, cols], m_ref.at[:, cols], in_sem.at[0, c])

    def z_copy(c):
        cols = pl.ds(pl.multiple_of(c * CB, CB), CB)
        return pltpu.make_async_copy(z_hbm.at[:, cols], parts.at[pl.ds(0, tokens), cols], in_sem.at[1, c])

    def dy_copy(c):
        cols = pl.ds(pl.multiple_of(c * CB, CB), CB)
        return pltpu.make_async_copy(dy_hbm.at[:, cols], parts.at[pl.ds(tokens, tokens), cols], in_sem.at[2, c])

    a_copy = pltpu.make_async_copy(a_hbm, a_v, a_sem)

    @pl.loop(0, nc)
    def _(c):
        e_copy(c).start()
        z_copy(c).start()
        dy_copy(c).start()

        @pl.when(c == nc // 2)
        def _():
            a_copy.start()

    qt = qt_ref[...]
    q_max = jnp.max(jnp.abs(qt), axis=1, keepdims=True)
    qs[...] = stack3((qt / q_max) * (1.0 / d_out))
    p_acc[...] = jnp.zeros_like(p_acc)
    h_acc[...] = jnp.zeros_like(h_acc)

    @pl.loop(0, nc)
    def _(c):
        e_copy(c).wait()
        z_copy(c).wait()
        dy_copy(c).wait()
        cols = pl.ds(pl.multiple_of(c * CB, CB), CB)
        qc = qs[:, cols]
        for r in range(d_in // RB):
            rows = pl.ds(r * RB, RB)
            e1, e2, e3 = split3(m_ref[rows, cols])
            p_acc[:, rows] += (mm_nt(qc, e3) + mm_nt(qc, e2)) + mm_nt(qc, e1)
        for r in range(tokens // RB):
            rows = pl.ds(r * RB, RB)
            gb = gelu_grad(parts[rows, cols], parts[pl.ds(tokens + r * RB, RB), cols]).astype(BF16)
            g[rows, cols] = gb
            h_acc[:, rows] += mm_nt(qc, gb)

    a_copy.wait()
    hs = stack3(fold3(h_acc[...]))
    pt = (fold3(p_acc[...]) + fold3(mm(hs, a_v[...])) * (1.0 / tokens)) * q_max * float(d_out)
    for b in range(n_p):
        p_own[b] = pt[:, b * 128:(b + 1) * 128]

    pl.semaphore_wait(barrier, n - 1)

    def p_send(b):
        owner = base + 2 * b + 1
        return pltpu.make_async_remote_copy(
            src_ref=p_own.at[b], dst_ref=p_recv.at[lax.rem(me - owner + 2 * n - 1, n)],
            send_sem=ps_sem, recv_sem=pr_sem, device_id=(owner,), device_id_type=MESH)

    for b in range(n_p):
        @pl.when(me != base + 2 * b + 1)
        def _():
            p_send(b).start()

    at_v[...] = a_v[...].T

    def build(c):
        cols = pl.ds(pl.multiple_of(c * CB, CB), CB)
        for r in range(d_in // RB):
            rows = pl.ds(r * RB, RB)
            m = mm(at_v[rows, :], g[:, cols]) * (1.0 / tokens) + m_ref[rows, cols]
            m_ref[rows, cols] = m
            for i, part in enumerate(split3(m)):
                parts[pl.ds(i * d_in + r * RB, RB), cols] = part

    pl.loop(0, nc // 2)(build)

    def spread(buf, index, send_sem, recv_sem, k):
        return pltpu.make_async_remote_copy(
            src_ref=buf.at[index], dst_ref=buf.at[index], send_sem=send_sem, recv_sem=recv_sem,
            device_id=(lax.rem(me + k, n),), device_id_type=MESH)

    def bulk(ref, send_sem, recv_sem):
        return pltpu.make_async_remote_copy(
            src_ref=ref, dst_ref=ref, send_sem=send_sem, recv_sem=recv_sem, device_id=(me,), device_id_type=MESH)

    @pl.when(p_owner)
    def _():
        bulk(p_recv, ps_sem, pr_sem).wait_recv()
        p_all[p_mine] = p_own[p_mine] + jnp.sum(p_recv[...], axis=0)

        @pl.loop(1, n)
        def _(k):
            spread(p_all, p_mine, pbs_sem, pbr_sem.at[p_mine], k).start()

    pl.loop(nc // 2, nc)(build)

    for b in range(n_p):
        @pl.when(me != base + 2 * b + 1)
        def _():
            bulk(p_all.at[b], pbs_sem, pbr_sem.at[b]).wait_recv()

    p = orthonormalize(jnp.concatenate([p_all[b] for b in range(n_p)], axis=1))
    pt_ref[...] = p
    ps = stack3(p)

    def y_send(t):
        owner = base + t
        return pltpu.make_async_remote_copy(
            src_ref=y_own.at[t], dst_ref=y_recv.at[lax.rem(me - owner + 2 * n - 1, n)],
            send_sem=ys_sem, recv_sem=yr_sem, device_id=(owner,), device_id_type=MESH)

    @pl.loop(0, n_y // 2)
    def _(s):
        for i in range(2):
            t = 2 * s + i
            cols = pl.ds(pl.multiple_of(t * cw, cw), cw)
            y = mm(ps, parts[pl.ds(2 * d_in, d_in), cols]) + mm(ps, parts[pl.ds(d_in, d_in), cols])
            y_own[t] = fold3(y + mm(ps, parts[pl.ds(0, d_in), cols]))
        for i in range(2):
            t = 2 * s + i

            @pl.when(me != base + t)
            def _():
                y_send(t).start()

    p1, p2, p3 = [x.astype(F32) for x in split3(p)]
    fill = jnp.zeros((128 - 9 * RANK, d_in), F32)
    pleft_ref[...] = jnp.concatenate([p1] * 3 + [p2] * 3 + [p3] * 3 + [fill], axis=0).T.astype(BF16)

    @pl.when(y_owner)
    def _():
        bulk(y_recv, ys_sem, yr_sem).wait_recv()
        q_ref[y_mine] = (y_own[y_mine] + jnp.sum(y_recv[...], axis=0)) * (1.0 / n)

        @pl.loop(1, n)
        def _(k):
            spread(q_ref, y_mine, ybs_sem, ybr_sem.at[y_mine], k).start()

    for t in range(n_y):
        @pl.when(me != base + t)
        def _():
            bulk(q_ref.at[t], ybs_sem, ybr_sem.at[t]).wait_recv()

    @pl.when(p_owner)
    def _():
        bulk(p_own.at[pl.ds(0, n_p - 1)], ps_sem, pr_sem).wait_send()
        bulk(p_recv, pbs_sem, pr_sem).wait_send()

    @pl.when(jnp.logical_not(p_owner))
    def _():
        bulk(p_own, ps_sem, pr_sem).wait_send()

    @pl.when(y_owner)
    def _():
        bulk(y_own.at[pl.ds(0, n_y - 1)], ys_sem, yr_sem).wait_send()
        bulk(y_recv, ybs_sem, yr_sem).wait_send()

    @pl.when(jnp.logical_not(y_owner))
    def _():
        bulk(y_own, ys_sem, yr_sem).wait_send()


def apply_kernel(pleft_ref, pt_ref, q_ref, m_ref, p_out, q_out, e_out, qr, qt, stage, sem, e_sem):
    d_in, d_out = m_ref.shape
    n_y, _, cw = q_ref.shape
    p_copy = pltpu.make_async_copy(pt_ref, p_out, sem.at[0])
    p_copy.start()
    fill = jnp.zeros((128 - 9 * RANK, cw), F32)
    for t in range(n_y):
        q = q_ref[t]
        qt[:, t * cw:(t + 1) * cw] = q
        three = [x.astype(F32) for x in split3(q)]
        qr[:, t * cw:(t + 1) * cw] = jnp.concatenate(three * 3 + [fill], axis=0).astype(BF16)
    q_copy = pltpu.make_async_copy(qt, q_out, sem.at[1])
    q_copy.start()

    def e_copy(c):
        cols = pl.ds(pl.multiple_of(c * CB, CB), CB)
        return pltpu.make_async_copy(stage.at[:, cols], e_out.at[0, :, cols], e_sem.at[c])

    @pl.loop(0, d_out // CB)
    def _(c):
        cols = pl.ds(pl.multiple_of(c * CB, CB), CB)
        qc = qr[:, cols]
        for r in range(d_in // RB):
            rows = pl.ds(r * RB, RB)
            stage[rows, cols] = m_ref[rows, cols] - mm(pleft_ref[rows, :], qc)
        e_copy(c).start()

    p_copy.wait()
    q_copy.wait()

    @pl.loop(0, d_out // CB)
    def _(c):
        e_copy(c).wait()


def solution(mesh):
    n = mesh.shape["data"]

    def per_device(act_in, pre_act, grad_out, q_init, err_mem):
        tokens, d_in = act_in.shape
        d_out = pre_act.shape[1]
        nc, n_p, n_y = d_out // CB, d_in // 128, n // 2
        cw = d_out // n_y
        hbm = pl.BlockSpec(memory_space=pltpu.HBM)
        vmem = pl.BlockSpec(memory_space=pltpu.VMEM)
        pleft, pt, q, m = pl.pallas_call(
            functools.partial(reduce_kernel, n),
            out_shape=(
                pltpu.VMEM((d_in, 128), BF16),
                pltpu.VMEM((RANK, d_in), F32),
                pltpu.VMEM((n_y, RANK, cw), F32),
                pltpu.VMEM((d_in, d_out), F32),
            ),
            in_specs=[hbm, hbm, hbm, vmem, hbm],
            out_specs=(vmem,) * 4,
            scratch_shapes=[
                pltpu.VMEM((3 * d_in, d_out), BF16),
                pltpu.VMEM((tokens, d_out), BF16),
                pltpu.VMEM((tokens, d_in), BF16),
                pltpu.VMEM((d_in, tokens), BF16),
                pltpu.VMEM((32, d_out), BF16),
                pltpu.VMEM((32, d_in), F32),
                pltpu.VMEM((32, tokens), F32),
                pltpu.VMEM((n_p, RANK, 128), F32),
                pltpu.VMEM((n - 1, RANK, 128), F32),
                pltpu.VMEM((n_p, RANK, 128), F32),
                pltpu.VMEM((n_y, RANK, cw), F32),
                pltpu.VMEM((n - 1, RANK, cw), F32),
                pltpu.SemaphoreType.DMA((3, nc)),
                pltpu.SemaphoreType.DMA,
                pltpu.SemaphoreType.DMA,
                pltpu.SemaphoreType.DMA,
                pltpu.SemaphoreType.DMA,
                pltpu.SemaphoreType.DMA((n_p,)),
                pltpu.SemaphoreType.DMA,
                pltpu.SemaphoreType.DMA,
                pltpu.SemaphoreType.DMA,
                pltpu.SemaphoreType.DMA((n_y,)),
            ],
            compiler_params=pltpu.CompilerParams(
                collective_id=0, has_side_effects=True, vmem_limit_bytes=42 * 1024 * 1024),
            name="reduce_kernel",
        )(act_in, pre_act, grad_out, q_init.T, err_mem)
        p_t, q_t, err_new = pl.pallas_call(
            apply_kernel,
            out_shape=(
                jax.ShapeDtypeStruct((RANK, d_in), F32),
                jax.ShapeDtypeStruct((RANK, d_out), F32),
                jax.ShapeDtypeStruct((1, d_in, d_out), F32),
            ),
            in_specs=[vmem] * 4,
            out_specs=(hbm,) * 3,
            scratch_shapes=[
                pltpu.VMEM((128, d_out), BF16),
                pltpu.VMEM((RANK, d_out), F32),
                pltpu.VMEM((d_in, d_out), F32),
                pltpu.SemaphoreType.DMA((2,)),
                pltpu.SemaphoreType.DMA((nc,)),
            ],
            compiler_params=pltpu.CompilerParams(vmem_limit_bytes=24 * 1024 * 1024),
            name="apply_kernel",
        )(pleft, pt, q, m)
        return p_t.T, q_t.T, err_new

    return jax.shard_map(
        per_device, mesh=mesh,
        in_specs=(P("data", None), P("data", None), P("data", None), P(None, None), P("data", None, None)),
        out_specs=(P(None, None), P(None, None), P("data", None, None)), check_vma=False)
```

time: 302 us -> 50.5 us (0.17)
  waiting for transfers between devices: 128 us -> 0 us
  matrix products: 74.7 us -> 0 us
  Pallas kernels: 0 us -> 49.7 us
  blocking collectives: 42.2 us -> 0 us
  local copies, waits for them, and re-layouts: 36 us -> 0 us
  between operations: 14.1 us -> 0.64 us
  loops' own time: 5.79 us -> 0 us
    psum x1 -> x0, waiting for transfers between devices: 127 us -> none  [per_device(): q_factor = lax.psum(q_part, 'data') / group_size]
    dot_general x20 -> x0, matrix products: 74.7 us -> none  [the longest x1 18.4 us: per_device(): lax.dot_general(p_factor, q_factor, (((1,), (1,)), ((), ())), precision=E...]
    pallas_call x0 -> x2, Pallas kernels: none -> 49.7 us  [the longest x1 43.4 us: per_device(): pl.pallas_call(functools.partial(reduce_kernel, n), out_shape=(pltpu.VMEM...]
    psum x1 -> x0, blocking collectives: 42.2 us -> none  [per_device(): p_sum = lax.psum(p_part, 'data')]
    unnamed x12 -> x0, local copies, waits for them, and re-layouts: 35.1 us -> none
    another operation x1 -> x0, loops' own time: 5.79 us -> none  [orthonormalize(): return lax.fori_loop(0, p_sum.shape[1], gs_step, jnp.zeros_like(p_sum))]
  transfers between devices with their start and end apart: 1 -> 0, of which waited for: 1 -> 0; matrix products, arithmetic and copies ran while one was open for 0% -> 0% of each run, Pallas kernels for 0% -> 0%
where the time goes in v1:
time: 50.5 us; the launch traced here: 50.4 us
  Pallas kernels  49.7 us (98%)
  between operations  0.64 us (1%)
    pallas_call x1, Pallas kernels, per_device(): pl.pallas_call(functools.partial(reduce_kernel, n), out_shape=(pltpu.VMEM...  43.4 us
    pallas_call x1, Pallas kernels, per_device(): pl.pallas_call(apply_kernel, out_shape=(jax.ShapeDtypeStruct((RANK, d_in)...  6.35 us

profile of v1, /device:TPU:0, one launch (start us, length us, event | category | flops | bytes accessed | tf_op | source)
XLA Modules:
  0.0 50.4 jit_solution(15194492207422830758)
XLA Ops:
  0.6 43.4 %reduce_kernel.1 = (bf16[1024,128]{1,0:T(8,128)(2,1)S(1)}, f32[8,1024]{1,0:T(8,128)S(1)}, f32[16,8,256]{2,1,0:T(8,128)S(1)}, f32[1024,4096]{1,0:T(8,128)S(1)}) custom-call(bf16[512,1024]{1,0:T(8,128)(2,1)} %a_hbm.1, bf16[512,4096]{1,0:T(8,128)(2,1)} %z_hbm.1, bf16[512,4096]{1,0:T(8,128)(2,1)} %dy_hbm.1, f32[8,4096]{1,0:T(8,128)} %bitcast.3, ...), custom_call_target="tpu_custom_call" | custom-call | tf_op jit(solution)/shard_map/reduce_kernel/pallas_call | solution.py:301
  44.0 6.4 %apply_kernel.1 = (f32[8,1024]{1,0:T(8,128)}, f32[8,4096]{1,0:T(8,128)}, f32[1,1024,4096]{2,1,0:T(8,128)}) custom-call(bf16[1024,128]{1,0:T(8,128)(2,1)S(1)} %get-tuple-element.10.pleft_ref, f32[8,1024]{1,0:T(8,128)S(1)} %get-tuple-element.11.pt_ref, f32[16,8,256]{2,1,0:T(8,128)S(1)} %get-tuple-element.12.q_ref, f32[1024,4096]{1,0:T(8,128)S(1)} %get-tuple-element.13.m_ref), custom_call_target="tpu_custom_call" | custom-call | tf_op jit(solution)/shard_map/apply_kernel/pallas_call | solution.py:339

commit v2 on v1

v2 whole, which is shorter than its diff:
```python
import functools

import jax
import jax.numpy as jnp
from jax import lax
from jax.experimental import pallas as pl
from jax.experimental.pallas import tpu as pltpu
from jax.sharding import PartitionSpec as P

F32 = jnp.float32
BF16 = jnp.bfloat16
MESH = pl.DeviceIdType.MESH
RANK = 8
CB = 256
RB = 256
NT = (((1,), (1,)), ((), ()))


def split3(x):
    hi = x.astype(BF16)
    rest = x - hi.astype(F32)
    mid = rest.astype(BF16)
    low = (rest - mid.astype(F32)).astype(BF16)
    return hi, mid, low


def stack3(x):
    parts = [p.astype(F32) for p in split3(x)]
    return jnp.concatenate(parts + [jnp.zeros_like(x)], axis=0).astype(BF16)


def fold3(y):
    return (y[16:24] + y[8:16]) + y[0:8]


def mm(a, b):
    return jnp.dot(a, b, preferred_element_type=F32)


def mm_nt(a, b):
    return lax.dot_general(a, b, NT, preferred_element_type=F32)


def gelu_grad(z, dy):
    c = 0.7978845608028654
    x = z.astype(F32)
    x2 = x * x
    t = jnp.tanh(x * (x2 * (c * 0.044715) + c))
    up = 1.0 + t
    slope = ((x * up) * (1.0 - t)) * (x2 * (1.5 * c * 0.044715) + 0.5 * c)
    return (0.5 * up + slope) * dy.astype(F32)


def orthonormalize(p):
    row = lax.broadcasted_iota(jnp.int32, (RANK, 1), 0)
    w = p
    norm2 = jnp.zeros((RANK, 1), F32)
    for j in range(RANK):
        v = w[j:j + 1]
        d = jnp.sum(jnp.where(row > j, p, w) * v, axis=1, keepdims=True)
        norm2 = jnp.where(row == j, d, norm2)
        if j + 1 < RANK:
            coef = jnp.where(row > j, d / d[j:j + 1], 0.0)
            w = w - coef * v
    return w / jnp.sqrt(norm2)


def far_first():
    places = [(i, fy, fx, fc) for i in range(4) for fy in range(2) for fx in range(2) for fc in range(2)]
    places.remove((3, 0, 0, 0))
    return sorted(places, key=lambda p: -((2, 1, 1, 0)[p[0]] + p[1] + p[2]))


def reduce_kernel(n, a_hbm, z_hbm, dy_hbm, qt_hbm, e_hbm, pleft_ref, pt_ref, q_ref, m_ref,
                  parts, g, z_v, dy_v, a_v, at_v, qt_v, qs, p_acc, h_acc, p_own, p_recv, p_all,
                  y_mate, y_own, y_recv,
                  in_sem, q_sem, a_sem, ps_sem, pr_sem, pbs_sem, pbr_sem,
                  ms_sem, mr_sem, ys_sem, yr_sem, ybs_sem, ybr_sem):
    me = lax.axis_index("data")
    d_in, d_out = m_ref.shape
    tokens = z_v.shape[0]
    n_p = d_in // 128
    n_half = y_own.shape[0]
    cw = d_out // (2 * n_half)
    core = lax.rem(me, 2)
    fx = lax.rem(lax.div(me, 2), 2)
    fy = lax.rem(lax.div(me, 4), 2)
    fz = lax.div(me, 8)
    central = (fz >= 1) & (fz <= 2)
    mine = jnp.minimum(jnp.maximum(fz - 1, 0), 1) + 2 * (fx + 2 * fy)

    def owner_chip(s):
        return 4 * (1 + lax.rem(s, 2)) + lax.div(s, 2)

    barrier = pltpu.get_barrier_semaphore()

    def e_copy(c):
        cols = pl.ds(pl.multiple_of(c * CB, CB), CB)
        return pltpu.make_async_copy(e_hbm.at[0, :, cols], m_ref.at[:, cols], in_sem.at[c])

    def z_copy(c):
        cols = pl.ds(pl.multiple_of(c * CB, CB), CB)
        return pltpu.make_async_copy(z_hbm.at[:, cols], z_v.at[:, cols], in_sem.at[c])

    def dy_copy(c):
        cols = pl.ds(pl.multiple_of(c * CB, CB), CB)
        return pltpu.make_async_copy(dy_hbm.at[:, cols], dy_v.at[:, cols], in_sem.at[c])

    nc = d_out // CB
    q_copy = pltpu.make_async_copy(qt_hbm, qt_v, q_sem)
    a_copy = pltpu.make_async_copy(a_hbm, a_v, a_sem)
    q_copy.start()

    @pl.loop(0, nc)
    def _(c):
        z_copy(c).start()
        dy_copy(c).start()
        e_copy(c).start()

        @pl.when(c == nc // 2)
        def _():
            a_copy.start()

    @pl.loop(1, n)
    def _(k):
        pl.semaphore_signal(barrier, inc=1, device_id=(lax.rem(me + k, n),), device_id_type=MESH)

    p_acc[...] = jnp.zeros_like(p_acc)
    h_acc[...] = jnp.zeros_like(h_acc)
    q_copy.wait()
    qt = qt_v[...]
    q_max = jnp.max(jnp.abs(qt), axis=1, keepdims=True)
    qs[...] = stack3((qt / q_max) * (1.0 / d_out))

    def arrive(c):
        whole = parts.at[pl.ds(2 * c, 2), pl.ds(0, 2 * (d_in + tokens))]
        pltpu.make_async_copy(whole, whole, in_sem.at[c]).wait()

    def stream(first, count):
        for i in range(count):
            arrive(first + i)
        for i in range(count):
            c = first + i
            cols = pl.ds(pl.multiple_of(c * CB, CB), CB)
            qc = qs[:, cols]
            for r in range(d_in // RB):
                rows = pl.ds(r * RB, RB)
                e1, e2, e3 = split3(m_ref[rows, cols])
                p_acc[:, rows] += (mm_nt(qc, e3) + mm_nt(qc, e2)) + mm_nt(qc, e1)
                if r % 2 == 1 and r // 2 < tokens // RB:
                    rows = pl.ds(r // 2 * RB, RB)
                    gb = gelu_grad(z_v[rows, cols], dy_v[rows, cols]).astype(BF16)
                    for h in range(CB // 128):
                        g[2 * c + h, rows, :] = gb[:, h * 128:(h + 1) * 128]
                    h_acc[:, rows] += mm_nt(qc, gb)

    stream(0, 1)

    @pl.loop(0, (nc - 2) // 2)
    def _(s):
        stream(1 + 2 * s, 2)

    stream(nc - 1, 1)

    a_copy.wait()
    hs = stack3(fold3(h_acc[...]))
    pt = (fold3(p_acc[...]) + fold3(mm(hs, a_v[...])) * (1.0 / tokens)) * q_max * float(d_out)
    for b in range(n_p):
        p_own[b] = pt[:, b * 128:(b + 1) * 128]

    pl.semaphore_wait(barrier, n - 1)

    def remote(src, dst, send_sem, recv_sem, device):
        return pltpu.make_async_remote_copy(
            src_ref=src, dst_ref=dst, send_sem=send_sem, recv_sem=recv_sem, device_id=(device,), device_id_type=MESH)

    def bulk(ref, send_sem, recv_sem):
        return remote(ref, ref, send_sem, recv_sem, me)

    def broadcast(buf, index, send_sem, recv_sem):
        for plane, gy, gx, gc in far_first():
            there = (3, 0, 2, 1)[plane]
            z = there * (2 - fz) + (3 - there) * (fz - 1)
            y = 1 - fy if gy else fy
            x = 1 - fx if gx else fx
            c = 1 - core if gc else core
            remote(buf.at[index], buf.at[index], send_sem, recv_sem, z * 8 + y * 4 + x * 2 + c).start()

    p_owner = central & (core == 1)

    @pl.loop(0, n_p)
    def _(b):
        owner = 2 * owner_chip(b) + 1

        @pl.when(me != owner)
        def _():
            remote(p_own.at[b], p_recv.at[lax.rem(me - owner + 2 * n - 1, n)], ps_sem, pr_sem, owner).start()

    @pl.loop(0, d_in // RB)
    def _(r):
        rows = pl.ds(pl.multiple_of(r * RB, RB), RB)
        at_v[rows, :] = a_v[:, rows].T

    def build(c):
        cols = pl.ds(pl.multiple_of(c * CB, CB), CB)
        gc = jnp.concatenate([g[2 * c + h] for h in range(CB // 128)], axis=1)
        for r in range(d_in // RB):
            rows = pl.ds(r * RB, RB)
            m = mm(at_v[rows, :], gc) * (1.0 / tokens) + m_ref[rows, cols]
            m_ref[rows, cols] = m
            for i, part in enumerate(split3(m)):
                for h in range(CB // 128):
                    parts[2 * c + h, pl.ds(i * d_in + r * RB, RB), :] = part[:, h * 128:(h + 1) * 128]

    pl.loop(0, nc // 2 + 1)(build)

    @pl.when(p_owner)
    def _():
        bulk(p_recv, ps_sem, pr_sem).wait_recv()
        p_all[mine] = p_own[mine] + jnp.sum(p_recv[...], axis=0)
        broadcast(p_all, mine, pbs_sem, pbr_sem)

    pl.loop(nc // 2 + 1, nc)(build)

    @pl.when(p_owner)
    def _():
        bulk(p_all.at[pl.ds(0, n_p - 1)], pbs_sem, pbr_sem).wait_recv()

    @pl.when(jnp.logical_not(p_owner))
    def _():
        bulk(p_all, pbs_sem, pbr_sem).wait_recv()

    p = orthonormalize(jnp.concatenate([p_all[b] for b in range(n_p)], axis=1))
    pt_ref[...] = p
    ps = stack3(p)

    def y_tile(t):
        def part(i):
            return jnp.concatenate(
                [parts[t * (cw // 128) + h, pl.ds(i * d_in, d_in), :] for h in range(cw // 128)], axis=1)
        y = mm(ps, part(2)) + mm(ps, part(1))
        return fold3(y + mm(ps, part(0)))

    mate = me + 1 - 2 * core

    @pl.loop(0, n_half // 2)
    def _(k):
        for i in range(2):
            s = 2 * k + i
            y_mate[s] = y_tile((1 - core) * n_half + s)
        for i in range(2):
            s = 2 * k + i
            remote(y_mate.at[s], y_mate.at[n_half + s], ms_sem, mr_sem.at[s], mate).start()

    @pl.loop(0, n_half // 2)
    def _(k):
        for i in range(2):
            s = 2 * k + i
            bulk(y_mate.at[n_half + s], ms_sem, mr_sem.at[s]).wait_recv()
        for i in range(2):
            s = 2 * k + i
            y_own[s] = y_tile(core * n_half + s) + y_mate[n_half + s]
        for i in range(2):
            s = 2 * k + i
            chip = owner_chip(s)
            slot = lax.rem(lax.div(me, 2) - chip + n - 1, n // 2)

            @pl.when(me != 2 * chip + core)
            def _():
                remote(y_own.at[s], y_recv.at[slot], ys_sem, yr_sem, 2 * chip + core).start()

    p1, p2, p3 = [x.astype(F32) for x in split3(p)]
    fill = jnp.zeros((128 - 9 * RANK, d_in), F32)
    pleft_ref[...] = jnp.concatenate([p1] * 3 + [p2] * 3 + [p3] * 3 + [fill], axis=0).T.astype(BF16)
    q_mine = core * n_half + mine

    @pl.when(central)
    def _():
        bulk(y_recv, ys_sem, yr_sem).wait_recv()
        q_ref[q_mine] = (y_own[mine] + jnp.sum(y_recv[...], axis=0)) * (1.0 / n)
        broadcast(q_ref, q_mine, ybs_sem, ybr_sem)

    bulk(y_mate.at[pl.ds(0, n_half)], ms_sem, yr_sem).wait_send()

    @pl.when(p_owner)
    def _():
        bulk(p_own.at[pl.ds(0, n_p - 1)], ps_sem, pr_sem).wait_send()
        bulk(p_recv, pbs_sem, pr_sem).wait_send()

    @pl.when(jnp.logical_not(p_owner))
    def _():
        bulk(p_own, ps_sem, pr_sem).wait_send()

    @pl.when(central)
    def _():
        bulk(y_own.at[pl.ds(0, n_half - 1)], ys_sem, yr_sem).wait_send()
        bulk(q_ref.at[pl.ds(0, 2 * n_half - 1)], ybs_sem, ybr_sem).wait_recv()
        bulk(parts.at[0, pl.ds(0, (n - 1) * RANK * cw // 64)], ybs_sem, yr_sem).wait_send()

    @pl.when(jnp.logical_not(central))
    def _():
        bulk(y_own, ys_sem, yr_sem).wait_send()
        bulk(q_ref, ybs_sem, ybr_sem).wait_recv()


def apply_kernel(pleft_ref, pt_ref, q_ref, m_ref, p_out, q_out, e_out, stage, p_sem, q_sem, e_sem):
    d_in, d_out = m_ref.shape
    n_y, _, cw = q_ref.shape
    p_copy = pltpu.make_async_copy(pt_ref, p_out, p_sem)
    fill = jnp.zeros((128 - 9 * RANK, cw), F32)

    def q_copy(c):
        cols = pl.ds(pl.multiple_of(c * cw, cw), cw)
        return pltpu.make_async_copy(q_ref.at[c], q_out.at[:, cols], q_sem)

    def e_copy(c):
        cols = pl.ds(pl.multiple_of(c * cw, cw), cw)
        return pltpu.make_async_copy(stage.at[:, cols], e_out.at[0, :, cols], e_sem)

    @pl.loop(0, n_y)
    def _(c):
        cols = pl.ds(pl.multiple_of(c * cw, cw), cw)
        three = [x.astype(F32) for x in split3(q_ref[c])]
        qc = jnp.concatenate(three * 3 + [fill], axis=0).astype(BF16)
        for r in range(d_in // RB):
            rows = pl.ds(r * RB, RB)
            stage[rows, cols] = m_ref[rows, cols] - mm(pleft_ref[rows, :], qc)
        e_copy(c).start()

    p_copy.start()

    @pl.loop(0, n_y)
    def _(c):
        q_copy(c).start()

    p_copy.wait()
    pltpu.make_async_copy(q_ref, q_ref, q_sem).wait()
    pltpu.make_async_copy(stage, e_out.at[0], e_sem).wait()


def solution(mesh):
    n = mesh.shape["data"]

    def per_device(act_in, pre_act, grad_out, q_init, err_mem):
        tokens, d_in = act_in.shape
        d_out = pre_act.shape[1]
        nc, n_p, n_y = d_out // CB, d_in // 128, n // 2
        cw = d_out // n_y
        hbm = pl.BlockSpec(memory_space=pltpu.HBM)
        vmem = pl.BlockSpec(memory_space=pltpu.VMEM)
        pleft, pt, q, m = pl.pallas_call(
            functools.partial(reduce_kernel, n),
            out_shape=(
                pltpu.VMEM((d_in, 128), BF16),
                pltpu.VMEM((RANK, d_in), F32),
                pltpu.VMEM((n_y, RANK, cw), F32),
                pltpu.VMEM((d_in, d_out), F32),
            ),
            in_specs=[hbm] * 5,
            out_specs=(vmem,) * 4,
            scratch_shapes=[
                pltpu.VMEM((d_out // 128, 3 * d_in, 128), BF16),
                pltpu.VMEM((d_out // 128, tokens, 128), BF16),
                pltpu.VMEM((tokens, d_out), BF16),
                pltpu.VMEM((tokens, d_out), BF16),
                pltpu.VMEM((tokens, d_in), BF16),
                pltpu.VMEM((d_in, tokens), BF16),
                pltpu.VMEM((RANK, d_out), F32),
                pltpu.VMEM((32, d_out), BF16),
                pltpu.VMEM((32, d_in), F32),
                pltpu.VMEM((32, tokens), F32),
                pltpu.VMEM((n_p, RANK, 128), F32),
                pltpu.VMEM((n - 1, RANK, 128), F32),
                pltpu.VMEM((n_p, RANK, 128), F32),
                pltpu.VMEM((n_y, RANK, cw), F32),
                pltpu.VMEM((n_y // 2, RANK, cw), F32),
                pltpu.VMEM((n // 2 - 1, RANK, cw), F32),
                pltpu.SemaphoreType.DMA((nc,)),
            ] + [pltpu.SemaphoreType.DMA] * 7 + [pltpu.SemaphoreType.DMA((n_y // 2,))]
            + [pltpu.SemaphoreType.DMA] * 4,
            compiler_params=pltpu.CompilerParams(
                collective_id=0, has_side_effects=True, vmem_limit_bytes=46 * 1024 * 1024),
            name="reduce_kernel",
        )(act_in, pre_act, grad_out, q_init.T, err_mem)
        p_t, q_t, err_new = pl.pallas_call(
            apply_kernel,
            out_shape=(
                jax.ShapeDtypeStruct((RANK, d_in), F32),
                jax.ShapeDtypeStruct((RANK, d_out), F32),
                jax.ShapeDtypeStruct((1, d_in, d_out), F32),
            ),
            in_specs=[vmem] * 4,
            out_specs=(hbm,) * 3,
            scratch_shapes=[
                pltpu.VMEM((d_in, d_out), F32),
            ] + [pltpu.SemaphoreType.DMA] * 3,
            compiler_params=pltpu.CompilerParams(vmem_limit_bytes=24 * 1024 * 1024),
            name="apply_kernel",
        )(pleft, pt, q, m)
        return p_t.T, q_t.T, err_new

    return jax.shard_map(
        per_device, mesh=mesh,
        in_specs=(P("data", None), P("data", None), P("data", None), P(None, None), P("data", None, None)),
        out_specs=(P(None, None), P(None, None), P("data", None, None)), check_vma=False)
```

time: 50.5 us -> 45.9 us (0.909)
  Pallas kernels: 49.7 us -> 45.1 us
    pallas_call x1, Pallas kernels: 43.4 us -> 39 us  [per_device(): pl.pallas_call(functools.partial(reduce_kernel, n), out_shape=(pltpu.VMEM...]
where the time goes in v2:
time: 45.9 us; the launch traced here: 45.8 us
  Pallas kernels  45.1 us (98%)
  between operations  0.64 us (1%)
    pallas_call x1, Pallas kernels, per_device(): pl.pallas_call(functools.partial(reduce_kernel, n), out_shape=(pltpu.VMEM...  39 us
    pallas_call x1, Pallas kernels, per_device(): pl.pallas_call(apply_kernel, out_shape=(jax.ShapeDtypeStruct((RANK, d_in)...  6.13 us

profile of v2, /device:TPU:0, one launch (start us, length us, event | category | flops | bytes accessed | tf_op | source)
XLA Modules:
  0.0 45.8 jit_solution(610841127947962607)
XLA Ops:
  0.6 39.0 %reduce_kernel.1 = (bf16[1024,128]{1,0:T(8,128)(2,1)S(1)}, f32[8,1024]{1,0:T(8,128)S(1)}, f32[16,8,256]{2,1,0:T(8,128)S(1)}, f32[1024,4096]{1,0:T(8,128)S(1)}) custom-call(bf16[512,1024]{1,0:T(8,128)(2,1)} %a_hbm.1, bf16[512,4096]{1,0:T(8,128)(2,1)} %z_hbm.1, bf16[512,4096]{1,0:T(8,128)(2,1)} %dy_hbm.1, f32[8,4096]{1,0:T(8,128)} %bitcast.3, ...), custom_call_target="tpu_custom_call" | custom-call | tf_op jit(solution)/shard_map/reduce_kernel/pallas_call | solution.py:351
  39.6 6.1 %apply_kernel.1 = (f32[8,1024]{1,0:T(8,128)}, f32[8,4096]{1,0:T(8,128)}, f32[1,1024,4096]{2,1,0:T(8,128)}) custom-call(bf16[1024,128]{1,0:T(8,128)(2,1)S(1)} %get-tuple-element.10.pleft_ref, f32[8,1024]{1,0:T(8,128)S(1)} %get-tuple-element.11.pt_ref, f32[16,8,256]{2,1,0:T(8,128)S(1)} %get-tuple-element.12.q_ref, f32[1024,4096]{1,0:T(8,128)S(1)} %get-tuple-element.13.m_ref), custom_call_target="tpu_custom_call" | custom-call | tf_op jit(solution)/shard_map/apply_kernel/pallas_call | solution.py:385

commit v3 on v2

--- a/solution.py
+++ b/solution.py
@@ -63,12 +63,6 @@
             coef = jnp.where(row > j, d / d[j:j + 1], 0.0)
             w = w - coef * v
     return w / jnp.sqrt(norm2)
-
-
-def far_first():
-    places = [(i, fy, fx, fc) for i in range(4) for fy in range(2) for fx in range(2) for fc in range(2)]
-    places.remove((3, 0, 0, 0))
-    return sorted(places, key=lambda p: -((2, 1, 1, 0)[p[0]] + p[1] + p[2]))
 
 
 def reduce_kernel(n, a_hbm, z_hbm, dy_hbm, qt_hbm, e_hbm, pleft_ref, pt_ref, q_ref, m_ref,
@@ -86,11 +80,17 @@
     fx = lax.rem(lax.div(me, 2), 2)
     fy = lax.rem(lax.div(me, 4), 2)
     fz = lax.div(me, 8)
-    central = (fz >= 1) & (fz <= 2)
-    mine = jnp.minimum(jnp.maximum(fz - 1, 0), 1) + 2 * (fx + 2 * fy)
-
-    def owner_chip(s):
-        return 4 * (1 + lax.rem(s, 2)) + lax.div(s, 2)
+    place = fx + 2 * fy
+    p_owner = (fz >= 2) & (core == 1)
+    p_mine = jnp.minimum(jnp.maximum(fz - 2, 0), 1) + 2 * place
+    y_owner = fz <= 1
+    y_mine = jnp.maximum(1 - fz, 0) + 2 * (3 - place)
+
+    def p_chip(b):
+        return 4 * (2 + lax.rem(b, 2)) + lax.div(b, 2)
+
+    def y_chip(s):
+        return 4 * (1 - lax.rem(s, 2)) + 3 - lax.div(s, 2)
 
     barrier = pltpu.get_barrier_semaphore()
 
@@ -177,20 +177,18 @@
     def bulk(ref, send_sem, recv_sem):
         return remote(ref, ref, send_sem, recv_sem, me)
 
-    def broadcast(buf, index, send_sem, recv_sem):
-        for plane, gy, gx, gc in far_first():
-            there = (3, 0, 2, 1)[plane]
-            z = there * (2 - fz) + (3 - there) * (fz - 1)
-            y = 1 - fy if gy else fy
-            x = 1 - fx if gx else fx
-            c = 1 - core if gc else core
-            remote(buf.at[index], buf.at[index], send_sem, recv_sem, z * 8 + y * 4 + x * 2 + c).start()
-
-    p_owner = central & (core == 1)
+    def broadcast(buf, index, send_sem, recv_sem, planes):
+        for z in planes:
+            for low in range(8):
+                there = 8 * z + low
+
+                @pl.when(me != there)
+                def _():
+                    remote(buf.at[index], buf.at[index], send_sem, recv_sem, there).start()
 
     @pl.loop(0, n_p)
     def _(b):
-        owner = 2 * owner_chip(b) + 1
+        owner = 2 * p_chip(b) + 1
 
         @pl.when(me != owner)
         def _():
@@ -212,15 +210,16 @@
                 for h in range(CB // 128):
                     parts[2 * c + h, pl.ds(i * d_in + r * RB, RB), :] = part[:, h * 128:(h + 1) * 128]
 
-    pl.loop(0, nc // 2 + 1)(build)
+    early = jnp.minimum(2 + 3 * ((1 - fx) + (1 - fy) + (3 - fz)), nc)
+    pl.loop(0, early)(build)
 
     @pl.when(p_owner)
     def _():
         bulk(p_recv, ps_sem, pr_sem).wait_recv()
-        p_all[mine] = p_own[mine] + jnp.sum(p_recv[...], axis=0)
-        broadcast(p_all, mine, pbs_sem, pbr_sem)
-
-    pl.loop(nc // 2 + 1, nc)(build)
+        p_all[p_mine] = p_own[p_mine] + jnp.sum(p_recv[...], axis=0)
+        broadcast(p_all, p_mine, pbs_sem, pbr_sem, (0, 3, 1, 2))
+
+    pl.loop(early, nc)(build)
 
     @pl.when(p_owner)
     def _():
@@ -262,7 +261,7 @@
             y_own[s] = y_tile(core * n_half + s) + y_mate[n_half + s]
         for i in range(2):
             s = 2 * k + i
-            chip = owner_chip(s)
+            chip = y_chip(s)
             slot = lax.rem(lax.div(me, 2) - chip + n - 1, n // 2)
 
             @pl.when(me != 2 * chip + core)
@@ -272,13 +271,13 @@
     p1, p2, p3 = [x.astype(F32) for x in split3(p)]
     fill = jnp.zeros((128 - 9 * RANK, d_in), F32)
     pleft_ref[...] = jnp.concatenate([p1] * 3 + [p2] * 3 + [p3] * 3 + [fill], axis=0).T.astype(BF16)
-    q_mine = core * n_half + mine
-
-    @pl.when(central)
+    q_mine = core * n_half + y_mine
+
+    @pl.when(y_owner)
     def _():
         bulk(y_recv, ys_sem, yr_sem).wait_recv()
-        q_ref[q_mine] = (y_own[mine] + jnp.sum(y_recv[...], axis=0)) * (1.0 / n)
-        broadcast(q_ref, q_mine, ybs_sem, ybr_sem)
+        q_ref[q_mine] = (y_own[y_mine] + jnp.sum(y_recv[...], axis=0)) * (1.0 / n)
+        broadcast(q_ref, q_mine, ybs_sem, ybr_sem, range(4))
 
     bulk(y_mate.at[pl.ds(0, n_half)], ms_sem, yr_sem).wait_send()
 
@@ -291,13 +290,13 @@
     def _():
         bulk(p_own, ps_sem, pr_sem).wait_send()
 
-    @pl.when(central)
+    @pl.when(y_owner)
     def _():
         bulk(y_own.at[pl.ds(0, n_half - 1)], ys_sem, yr_sem).wait_send()
         bulk(q_ref.at[pl.ds(0, 2 * n_half - 1)], ybs_sem, ybr_sem).wait_recv()
         bulk(parts.at[0, pl.ds(0, (n - 1) * RANK * cw // 64)], ybs_sem, yr_sem).wait_send()
 
-    @pl.when(jnp.logical_not(central))
+    @pl.when(jnp.logical_not(y_owner))
     def _():
         bulk(y_own, ys_sem, yr_sem).wait_send()
         bulk(q_ref, ybs_sem, ybr_sem).wait_recv()

time: 45.9 us -> 48.2 us (1.050)
  Pallas kernels: 45.1 us -> 47.1 us
    pallas_call x1, Pallas kernels: 39 us -> 41 us  [per_device(): pl.pallas_call(functools.partial(reduce_kernel, n), out_shape=(pltpu.VMEM...]
where the time goes in v3:
time: 48.2 us; the launch traced here: 47.8 us
  Pallas kernels  47.1 us (98%)
  between operations  0.64 us (1%)
    pallas_call x1, Pallas kernels, per_device(): pl.pallas_call(functools.partial(reduce_kernel, n), out_shape=(pltpu.VMEM...  41 us
    pallas_call x1, Pallas kernels, per_device(): pl.pallas_call(apply_kernel, out_shape=(jax.ShapeDtypeStruct((RANK, d_in)...  6.14 us

profile of v3, /device:TPU:0, one launch (start us, length us, event | category | flops | bytes accessed | tf_op | source)
XLA Modules:
  0.0 47.8 jit_solution(11066010024466398355)
XLA Ops:
  0.6 41.0 %reduce_kernel.1 = (bf16[1024,128]{1,0:T(8,128)(2,1)S(1)}, f32[8,1024]{1,0:T(8,128)S(1)}, f32[16,8,256]{2,1,0:T(8,128)S(1)}, f32[1024,4096]{1,0:T(8,128)S(1)}) custom-call(bf16[512,1024]{1,0:T(8,128)(2,1)} %a_hbm.1, bf16[512,4096]{1,0:T(8,128)(2,1)} %z_hbm.1, bf16[512,4096]{1,0:T(8,128)(2,1)} %dy_hbm.1, f32[8,4096]{1,0:T(8,128)} %bitcast.3, ...), custom_call_target="tpu_custom_call" | custom-call | tf_op jit(solution)/shard_map/reduce_kernel/pallas_call | solution.py:350
  41.6 6.1 %apply_kernel.1 = (f32[8,1024]{1,0:T(8,128)}, f32[8,4096]{1,0:T(8,128)}, f32[1,1024,4096]{2,1,0:T(8,128)}) custom-call(bf16[1024,128]{1,0:T(8,128)(2,1)S(1)} %get-tuple-element.10.pleft_ref, f32[8,1024]{1,0:T(8,128)S(1)} %get-tuple-element.11.pt_ref, f32[16,8,256]{2,1,0:T(8,128)S(1)} %get-tuple-element.12.q_ref, f32[1024,4096]{1,0:T(8,128)S(1)} %get-tuple-element.13.m_ref), custom_call_target="tpu_custom_call" | custom-call | tf_op jit(solution)/shard_map/apply_kernel/pallas_call | solution.py:384

commit v4 on v3

--- a/solution.py
+++ b/solution.py
@@ -69,7 +69,7 @@
                   parts, g, z_v, dy_v, a_v, at_v, qt_v, qs, p_acc, h_acc, p_own, p_recv, p_all,
                   y_mate, y_own, y_recv,
                   in_sem, q_sem, a_sem, ps_sem, pr_sem, pbs_sem, pbr_sem,
-                  ms_sem, mr_sem, ys_sem, yr_sem, ybs_sem, ybr_sem):
+                  ms_sem, mr_sem, ys_sem, yr_sem, ybs_sem, ybr_sem, qs_sem, qm_sem):
     me = lax.axis_index("data")
     d_in, d_out = m_ref.shape
     tokens = z_v.shape[0]
@@ -83,14 +83,14 @@
     place = fx + 2 * fy
     p_owner = (fz >= 2) & (core == 1)
     p_mine = jnp.minimum(jnp.maximum(fz - 2, 0), 1) + 2 * place
-    y_owner = fz <= 1
-    y_mine = jnp.maximum(1 - fz, 0) + 2 * (3 - place)
+    y_owner = (fz >= 1) & (fz <= 2)
+    y_mine = jnp.minimum(jnp.maximum(2 - fz, 0), 1) + 2 * (3 - place)
 
     def p_chip(b):
         return 4 * (2 + lax.rem(b, 2)) + lax.div(b, 2)
 
     def y_chip(s):
-        return 4 * (1 - lax.rem(s, 2)) + 3 - lax.div(s, 2)
+        return 4 * (2 - lax.rem(s, 2)) + 3 - lax.div(s, 2)
 
     barrier = pltpu.get_barrier_semaphore()
 
@@ -277,8 +277,21 @@
     def _():
         bulk(y_recv, ys_sem, yr_sem).wait_recv()
         q_ref[q_mine] = (y_own[y_mine] + jnp.sum(y_recv[...], axis=0)) * (1.0 / n)
-        broadcast(q_ref, q_mine, ybs_sem, ybr_sem, range(4))
-
+        tile = q_ref.at[q_mine]
+        for chip in range(n // 2):
+            @pl.when(lax.div(me, 2) != chip)
+            def _():
+                remote(tile, tile, ybs_sem, ybr_sem.at[y_mine], 2 * chip + core).start()
+        remote(tile, tile, ybs_sem, qm_sem, mate).start()
+
+    for s in range(n_half):
+        @pl.when(lax.div(me, 2) != y_chip(s))
+        def _():
+            tile = q_ref.at[core * n_half + s]
+            bulk(tile, ybs_sem, ybr_sem.at[s]).wait_recv()
+            remote(tile, tile, qs_sem, qm_sem, mate).start()
+
+    bulk(q_ref.at[pl.ds(0, n_half)], qs_sem, qm_sem).wait_recv()
     bulk(y_mate.at[pl.ds(0, n_half)], ms_sem, yr_sem).wait_send()
 
     @pl.when(p_owner)
@@ -293,13 +306,13 @@
     @pl.when(y_owner)
     def _():
         bulk(y_own.at[pl.ds(0, n_half - 1)], ys_sem, yr_sem).wait_send()
-        bulk(q_ref.at[pl.ds(0, 2 * n_half - 1)], ybs_sem, ybr_sem).wait_recv()
-        bulk(parts.at[0, pl.ds(0, (n - 1) * RANK * cw // 64)], ybs_sem, yr_sem).wait_send()
+        bulk(q_ref, ybs_sem, qm_sem).wait_send()
+        bulk(q_ref.at[pl.ds(0, n_half - 1)], qs_sem, qm_sem).wait_send()
 
     @pl.when(jnp.logical_not(y_owner))
     def _():
         bulk(y_own, ys_sem, yr_sem).wait_send()
-        bulk(q_ref, ybs_sem, ybr_sem).wait_recv()
+        bulk(q_ref.at[pl.ds(0, n_half)], qs_sem, qm_sem).wait_send()
 
 
 def apply_kernel(pleft_ref, pt_ref, q_ref, m_ref, p_out, q_out, e_out, stage, p_sem, q_sem, e_sem):
@@ -376,7 +389,7 @@
                 pltpu.VMEM((n // 2 - 1, RANK, cw), F32),
                 pltpu.SemaphoreType.DMA((nc,)),
             ] + [pltpu.SemaphoreType.DMA] * 7 + [pltpu.SemaphoreType.DMA((n_y // 2,))]
-            + [pltpu.SemaphoreType.DMA] * 4,
+            + [pltpu.SemaphoreType.DMA] * 3 + [pltpu.SemaphoreType.DMA((n_y // 2,))] + [pltpu.SemaphoreType.DMA] * 2,
             compiler_params=pltpu.CompilerParams(
                 collective_id=0, has_side_effects=True, vmem_limit_bytes=46 * 1024 * 1024),
             name="reduce_kernel",

time: 48.2 us -> 46.6 us (0.967)
  Pallas kernels: 47.1 us -> 45.8 us
    pallas_call x1, Pallas kernels: 41 us -> 39.7 us  [per_device(): pl.pallas_call(functools.partial(reduce_kernel, n), out_shape=(pltpu.VMEM...]
where the time goes in v4:
time: 46.6 us; the launch traced here: 46.4 us
  Pallas kernels  45.8 us (98%)
  between operations  0.64 us (1%)
    pallas_call x1, Pallas kernels, per_device(): pl.pallas_call(functools.partial(reduce_kernel, n), out_shape=(pltpu.VMEM...  39.7 us
    pallas_call x1, Pallas kernels, per_device(): pl.pallas_call(apply_kernel, out_shape=(jax.ShapeDtypeStruct((RANK, d_in)...  6.14 us

profile of v4, /device:TPU:0, one launch (start us, length us, event | category | flops | bytes accessed | tf_op | source)
XLA Modules:
  0.0 46.4 jit_solution(8554587859742195516)
XLA Ops:
  0.6 39.7 %reduce_kernel.1 = (bf16[1024,128]{1,0:T(8,128)(2,1)S(1)}, f32[8,1024]{1,0:T(8,128)S(1)}, f32[16,8,256]{2,1,0:T(8,128)S(1)}, f32[1024,4096]{1,0:T(8,128)S(1)}) custom-call(bf16[512,1024]{1,0:T(8,128)(2,1)} %a_hbm.1, bf16[512,4096]{1,0:T(8,128)(2,1)} %z_hbm.1, bf16[512,4096]{1,0:T(8,128)(2,1)} %dy_hbm.1, f32[8,4096]{1,0:T(8,128)} %bitcast.3, ...), custom_call_target="tpu_custom_call" | custom-call | tf_op jit(solution)/shard_map/reduce_kernel/pallas_call | solution.py:363
  40.3 6.1 %apply_kernel.1 = (f32[8,1024]{1,0:T(8,128)}, f32[8,4096]{1,0:T(8,128)}, f32[1,1024,4096]{2,1,0:T(8,128)}) custom-call(bf16[1024,128]{1,0:T(8,128)(2,1)S(1)} %get-tuple-element.10.pleft_ref, f32[8,1024]{1,0:T(8,128)S(1)} %get-tuple-element.11.pt_ref, f32[16,8,256]{2,1,0:T(8,128)S(1)} %get-tuple-element.12.q_ref, f32[1024,4096]{1,0:T(8,128)S(1)} %get-tuple-element.13.m_ref), custom_call_target="tpu_custom_call" | custom-call | tf_op jit(solution)/shard_map/apply_kernel/pallas_call | solution.py:397

commit v5 on v4

--- a/solution.py
+++ b/solution.py
@@ -63,6 +63,16 @@
             coef = jnp.where(row > j, d / d[j:j + 1], 0.0)
             w = w - coef * v
     return w / jnp.sqrt(norm2)
+
+
+def far_first(near_planes, cores):
+    places = [(i, fy, fx, fc) for i in range(4) for fy in range(2) for fx in range(2) for fc in range(cores)]
+    places.remove((3, 0, 0, 0))
+    return sorted(places, key=lambda p: -(near_planes[p[0]] + p[1] + p[2]))
+
+
+def flip(bit, by):
+    return bit + by - 2 * bit * by
 
 
 def reduce_kernel(n, a_hbm, z_hbm, dy_hbm, qt_hbm, e_hbm, pleft_ref, pt_ref, q_ref, m_ref,
@@ -84,13 +94,7 @@
     p_owner = (fz >= 2) & (core == 1)
     p_mine = jnp.minimum(jnp.maximum(fz - 2, 0), 1) + 2 * place
     y_owner = (fz >= 1) & (fz <= 2)
-    y_mine = jnp.minimum(jnp.maximum(2 - fz, 0), 1) + 2 * (3 - place)
-
-    def p_chip(b):
-        return 4 * (2 + lax.rem(b, 2)) + lax.div(b, 2)
-
-    def y_chip(s):
-        return 4 * (2 - lax.rem(s, 2)) + 3 - lax.div(s, 2)
+    y_mine = jnp.minimum(jnp.maximum(fz - 1, 0), 1) + 2 * place
 
     barrier = pltpu.get_barrier_semaphore()
 
@@ -177,18 +181,15 @@
     def bulk(ref, send_sem, recv_sem):
         return remote(ref, ref, send_sem, recv_sem, me)
 
-    def broadcast(buf, index, send_sem, recv_sem, planes):
-        for z in planes:
-            for low in range(8):
-                there = 8 * z + low
-
-                @pl.when(me != there)
-                def _():
-                    remote(buf.at[index], buf.at[index], send_sem, recv_sem, there).start()
+    def chip_at(z, gy, gx):
+        return 4 * z + 2 * flip(fy, gy) + flip(fx, gx)
 
     @pl.loop(0, n_p)
-    def _(b):
-        owner = 2 * p_chip(b) + 1
+    def _(k):
+        gy, gx = 1 - lax.div(k, 4), 1 - lax.rem(lax.div(k, 2), 2)
+        half = lax.rem(k + fz, 2)
+        owner = 2 * chip_at(2 + half, gy, gx) + 1
+        b = half + 2 * (flip(fx, gx) + 2 * flip(fy, gy))
 
         @pl.when(me != owner)
         def _():
@@ -217,7 +218,10 @@
     def _():
         bulk(p_recv, ps_sem, pr_sem).wait_recv()
         p_all[p_mine] = p_own[p_mine] + jnp.sum(p_recv[...], axis=0)
-        broadcast(p_all, p_mine, pbs_sem, pbr_sem, (0, 3, 1, 2))
+        tile = p_all.at[p_mine]
+        for plane, gy, gx, gc in far_first((2.5, 1.5, 1, 0), 2):
+            z = (0, 3, 1, 2)[plane] * (3 - fz) + plane * (fz - 2)
+            remote(tile, tile, pbs_sem, pbr_sem, 2 * chip_at(z, gy, gx) + (1 - gc)).start()
 
     pl.loop(early, nc)(build)
 
@@ -242,26 +246,25 @@
 
     mate = me + 1 - 2 * core
 
+    def pair(k):
+        gy, gx = 1 - lax.div(k, 2), 1 - lax.rem(k, 2)
+        column = 2 * (flip(fx, gx) + 2 * flip(fy, gy))
+        return [(lax.rem(fz + i, 2) + column, chip_at(1 + lax.rem(fz + i, 2), gy, gx)) for i in range(2)]
+
     @pl.loop(0, n_half // 2)
     def _(k):
-        for i in range(2):
-            s = 2 * k + i
+        for s, _ in pair(k):
             y_mate[s] = y_tile((1 - core) * n_half + s)
-        for i in range(2):
-            s = 2 * k + i
+        for s, _ in pair(k):
             remote(y_mate.at[s], y_mate.at[n_half + s], ms_sem, mr_sem.at[s], mate).start()
 
     @pl.loop(0, n_half // 2)
     def _(k):
-        for i in range(2):
-            s = 2 * k + i
+        for s, _ in pair(k):
             bulk(y_mate.at[n_half + s], ms_sem, mr_sem.at[s]).wait_recv()
-        for i in range(2):
-            s = 2 * k + i
+        for s, _ in pair(k):
             y_own[s] = y_tile(core * n_half + s) + y_mate[n_half + s]
-        for i in range(2):
-            s = 2 * k + i
-            chip = y_chip(s)
+        for s, chip in pair(k):
             slot = lax.rem(lax.div(me, 2) - chip + n - 1, n // 2)
 
             @pl.when(me != 2 * chip + core)
@@ -278,14 +281,14 @@
         bulk(y_recv, ys_sem, yr_sem).wait_recv()
         q_ref[q_mine] = (y_own[y_mine] + jnp.sum(y_recv[...], axis=0)) * (1.0 / n)
         tile = q_ref.at[q_mine]
-        for chip in range(n // 2):
-            @pl.when(lax.div(me, 2) != chip)
-            def _():
-                remote(tile, tile, ybs_sem, ybr_sem.at[y_mine], 2 * chip + core).start()
+        for plane, gy, gx, _ in far_first((2, 1, 1, 0), 1):
+            there = (3, 0, 2, 1)[plane]
+            z = there * (2 - fz) + (3 - there) * (fz - 1)
+            remote(tile, tile, ybs_sem, ybr_sem.at[y_mine], 2 * chip_at(z, gy, gx) + core).start()
         remote(tile, tile, ybs_sem, qm_sem, mate).start()
 
     for s in range(n_half):
-        @pl.when(lax.div(me, 2) != y_chip(s))
+        @pl.when(jnp.logical_not(y_owner) | (y_mine != s))
         def _():
             tile = q_ref.at[core * n_half + s]
             bulk(tile, ybs_sem, ybr_sem.at[s]).wait_recv()

time: 46.6 us -> 46.5 us (level)
  no operation moved by 1% of the time
where the time goes in v5:
time: 46.5 us; the launch traced here: 46.4 us
  Pallas kernels  45.7 us (98%)
  between operations  0.64 us (1%)
    pallas_call x1, Pallas kernels, per_device(): pl.pallas_call(functools.partial(reduce_kernel, n), out_shape=(pltpu.VMEM...  39.6 us
    pallas_call x1, Pallas kernels, per_device(): pl.pallas_call(apply_kernel, out_shape=(jax.ShapeDtypeStruct((RANK, d_in)...  6.13 us

profile of v5, /device:TPU:0, one launch (start us, length us, event | category | flops | bytes accessed | tf_op | source)
XLA Modules:
  0.0 46.4 jit_solution(7415686386673159007)
XLA Ops:
  0.6 39.6 %reduce_kernel.1 = (bf16[1024,128]{1,0:T(8,128)(2,1)S(1)}, f32[8,1024]{1,0:T(8,128)S(1)}, f32[16,8,256]{2,1,0:T(8,128)S(1)}, f32[1024,4096]{1,0:T(8,128)S(1)}) custom-call(bf16[512,1024]{1,0:T(8,128)(2,1)} %a_hbm.1, bf16[512,4096]{1,0:T(8,128)(2,1)} %z_hbm.1, bf16[512,4096]{1,0:T(8,128)(2,1)} %dy_hbm.1, f32[8,4096]{1,0:T(8,128)} %bitcast.3, ...), custom_call_target="tpu_custom_call" | custom-call | tf_op jit(solution)/shard_map/reduce_kernel/pallas_call | solution.py:366
  40.2 6.1 %apply_kernel.1 = (f32[8,1024]{1,0:T(8,128)}, f32[8,4096]{1,0:T(8,128)}, f32[1,1024,4096]{2,1,0:T(8,128)}) custom-call(bf16[1024,128]{1,0:T(8,128)(2,1)S(1)} %get-tuple-element.10.pleft_ref, f32[8,1024]{1,0:T(8,128)S(1)} %get-tuple-element.11.pt_ref, f32[16,8,256]{2,1,0:T(8,128)S(1)} %get-tuple-element.12.q_ref, f32[1024,4096]{1,0:T(8,128)S(1)} %get-tuple-element.13.m_ref), custom_call_target="tpu_custom_call" | custom-call | tf_op jit(solution)/shard_map/apply_kernel/pallas_call | solution.py:400

commit v6 on v5

--- a/solution.py
+++ b/solution.py
@@ -12,6 +12,7 @@
 MESH = pl.DeviceIdType.MESH
 RANK = 8
 CB = 256
+AHEAD = 4
 RB = 256
 NT = (((1,), (1,)), ((), ()))
 
@@ -115,15 +116,13 @@
     a_copy = pltpu.make_async_copy(a_hbm, a_v, a_sem)
     q_copy.start()
 
-    @pl.loop(0, nc)
-    def _(c):
+    def fetch(c):
         z_copy(c).start()
         dy_copy(c).start()
         e_copy(c).start()
 
-        @pl.when(c == nc // 2)
-        def _():
-            a_copy.start()
+    for c in range(AHEAD):
+        fetch(c)
 
     @pl.loop(1, n)
     def _(k):
@@ -143,6 +142,11 @@
     def stream(first, count):
         for i in range(count):
             arrive(first + i)
+        for i in range(count):
+            if not isinstance(first, int) or first + AHEAD + i < nc:
+                @pl.when(first + AHEAD + i < nc)
+                def _():
+                    fetch(first + AHEAD + i)
         for i in range(count):
             c = first + i
             cols = pl.ds(pl.multiple_of(c * CB, CB), CB)
@@ -164,6 +168,7 @@
     def _(s):
         stream(1 + 2 * s, 2)
 
+    a_copy.start()
     stream(nc - 1, 1)
 
     a_copy.wait()

time: 46.5 us -> 47.6 us (1.024)
  Pallas kernels: 45.7 us -> 46.8 us
    pallas_call x1, Pallas kernels: 39.6 us -> 40.7 us  [per_device(): pl.pallas_call(functools.partial(reduce_kernel, n), out_shape=(pltpu.VMEM...]
where the time goes in v6:
time: 47.6 us; the launch traced here: 47.4 us
  Pallas kernels  46.8 us (98%)
  between operations  0.64 us (1%)
    pallas_call x1, Pallas kernels, per_device(): pl.pallas_call(functools.partial(reduce_kernel, n), out_shape=(pltpu.VMEM...  40.7 us
    pallas_call x1, Pallas kernels, per_device(): pl.pallas_call(apply_kernel, out_shape=(jax.ShapeDtypeStruct((RANK, d_in)...  6.13 us

profile of v6, /device:TPU:0, one launch (start us, length us, event | category | flops | bytes accessed | tf_op | source)
XLA Modules:
  0.0 47.4 jit_solution(6003918218494499624)
XLA Ops:
  0.6 40.7 %reduce_kernel.1 = (bf16[1024,128]{1,0:T(8,128)(2,1)S(1)}, f32[8,1024]{1,0:T(8,128)S(1)}, f32[16,8,256]{2,1,0:T(8,128)S(1)}, f32[1024,4096]{1,0:T(8,128)S(1)}) custom-call(bf16[512,1024]{1,0:T(8,128)(2,1)} %a_hbm.1, bf16[512,4096]{1,0:T(8,128)(2,1)} %z_hbm.1, bf16[512,4096]{1,0:T(8,128)(2,1)} %dy_hbm.1, f32[8,4096]{1,0:T(8,128)} %bitcast.3, ...), custom_call_target="tpu_custom_call" | custom-call | tf_op jit(solution)/shard_map/reduce_kernel/pallas_call | solution.py:371
  41.3 6.1 %apply_kernel.1 = (f32[8,1024]{1,0:T(8,128)}, f32[8,4096]{1,0:T(8,128)}, f32[1,1024,4096]{2,1,0:T(8,128)}) custom-call(bf16[1024,128]{1,0:T(8,128)(2,1)S(1)} %get-tuple-element.10.pleft_ref, f32[8,1024]{1,0:T(8,128)S(1)} %get-tuple-element.11.pt_ref, f32[16,8,256]{2,1,0:T(8,128)S(1)} %get-tuple-element.12.q_ref, f32[1024,4096]{1,0:T(8,128)S(1)} %get-tuple-element.13.m_ref), custom_call_target="tpu_custom_call" | custom-call | tf_op jit(solution)/shard_map/apply_kernel/pallas_call | solution.py:405

commit v7 on v5

--- a/solution.py
+++ b/solution.py
@@ -13,6 +13,7 @@
 RANK = 8
 CB = 256
 RB = 256
+SB = 128
 NT = (((1,), (1,)), ((), ()))
 
 
@@ -147,12 +148,13 @@
             c = first + i
             cols = pl.ds(pl.multiple_of(c * CB, CB), CB)
             qc = qs[:, cols]
-            for r in range(d_in // RB):
-                rows = pl.ds(r * RB, RB)
+            q3 = jnp.concatenate([qc] * 3, axis=1)
+            for r in range(d_in // SB):
+                rows = pl.ds(r * SB, SB)
                 e1, e2, e3 = split3(m_ref[rows, cols])
-                p_acc[:, rows] += (mm_nt(qc, e3) + mm_nt(qc, e2)) + mm_nt(qc, e1)
-                if r % 2 == 1 and r // 2 < tokens // RB:
-                    rows = pl.ds(r // 2 * RB, RB)
+                p_acc[:, rows] += mm_nt(q3, jnp.concatenate([e3, e2, e1], axis=1))
+                if r % 2 == 1 and r // 2 < tokens // SB:
+                    rows = pl.ds(r // 2 * SB, SB)
                     gb = gelu_grad(z_v[rows, cols], dy_v[rows, cols]).astype(BF16)
                     for h in range(CB // 128):
                         g[2 * c + h, rows, :] = gb[:, h * 128:(h + 1) * 128]

time: 46.5 us -> 47.8 us (1.028)
  Pallas kernels: 45.7 us -> 47 us
    pallas_call x1, Pallas kernels: 39.6 us -> 40.9 us  [per_device(): pl.pallas_call(functools.partial(reduce_kernel, n), out_shape=(pltpu.VMEM...]
where the time goes in v7:
time: 47.8 us; the launch traced here: 47.7 us
  Pallas kernels  47 us (98%)
  between operations  0.64 us (1%)
    pallas_call x1, Pallas kernels, per_device(): pl.pallas_call(functools.partial(reduce_kernel, n), out_shape=(pltpu.VMEM...  40.9 us
    pallas_call x1, Pallas kernels, per_device(): pl.pallas_call(apply_kernel, out_shape=(jax.ShapeDtypeStruct((RANK, d_in)...  6.13 us

profile of v7, /device:TPU:0, one launch (start us, length us, event | category | flops | bytes accessed | tf_op | source)
XLA Modules:
  0.0 47.7 jit_solution(13143201269687926975)
XLA Ops:
  0.6 40.9 %reduce_kernel.1 = (bf16[1024,128]{1,0:T(8,128)(2,1)S(1)}, f32[8,1024]{1,0:T(8,128)S(1)}, f32[16,8,256]{2,1,0:T(8,128)S(1)}, f32[1024,4096]{1,0:T(8,128)S(1)}) custom-call(bf16[512,1024]{1,0:T(8,128)(2,1)} %a_hbm.1, bf16[512,4096]{1,0:T(8,128)(2,1)} %z_hbm.1, bf16[512,4096]{1,0:T(8,128)(2,1)} %dy_hbm.1, f32[8,4096]{1,0:T(8,128)} %bitcast.3, ...), custom_call_target="tpu_custom_call" | custom-call | tf_op jit(solution)/shard_map/reduce_kernel/pallas_call | solution.py:368
  41.5 6.1 %apply_kernel.1 = (f32[8,1024]{1,0:T(8,128)}, f32[8,4096]{1,0:T(8,128)}, f32[1,1024,4096]{2,1,0:T(8,128)}) custom-call(bf16[1024,128]{1,0:T(8,128)(2,1)S(1)} %get-tuple-element.10.pleft_ref, f32[8,1024]{1,0:T(8,128)S(1)} %get-tuple-element.11.pt_ref, f32[16,8,256]{2,1,0:T(8,128)S(1)} %get-tuple-element.12.q_ref, f32[1024,4096]{1,0:T(8,128)S(1)} %get-tuple-element.13.m_ref), custom_call_target="tpu_custom_call" | custom-call | tf_op jit(solution)/shard_map/apply_kernel/pallas_call | solution.py:402

commit v8 on v5

--- a/solution.py
+++ b/solution.py
@@ -91,10 +91,12 @@
     fy = lax.rem(lax.div(me, 4), 2)
     fz = lax.div(me, 8)
     place = fx + 2 * fy
-    p_owner = (fz >= 2) & (core == 1)
-    p_mine = jnp.minimum(jnp.maximum(fz - 2, 0), 1) + 2 * place
-    y_owner = (fz >= 1) & (fz <= 2)
-    y_mine = jnp.minimum(jnp.maximum(fz - 1, 0), 1) + 2 * place
+    here = lax.div(me, 2)
+    last = n // 2 - 1
+    p_owner = (here >= last - 2) | (here == last - 4)
+    p_mine = 2 * jnp.minimum(last - here, n_p // 2 - 1) + core
+    y_owner = fz <= 1
+    y_mine = jnp.minimum(fz, 1) + 2 * place
 
     barrier = pltpu.get_barrier_semaphore()
 
@@ -186,10 +188,9 @@
 
     @pl.loop(0, n_p)
     def _(k):
-        gy, gx = 1 - lax.div(k, 4), 1 - lax.rem(lax.div(k, 2), 2)
-        half = lax.rem(k + fz, 2)
-        owner = 2 * chip_at(2 + half, gy, gx) + 1
-        b = half + 2 * (flip(fx, gx) + 2 * flip(fy, gy))
+        b = lax.rem(k + me, n_p)
+        near = lax.div(b, 2)
+        owner = 2 * (last - near - lax.div(near, 3)) + lax.rem(b, 2)
 
         @pl.when(me != owner)
         def _():
@@ -211,7 +212,7 @@
                 for h in range(CB // 128):
                     parts[2 * c + h, pl.ds(i * d_in + r * RB, RB), :] = part[:, h * 128:(h + 1) * 128]
 
-    early = jnp.minimum(2 + 3 * ((1 - fx) + (1 - fy) + (3 - fz)), nc)
+    early = jnp.where(here == last, 3, 6)
     pl.loop(0, early)(build)
 
     @pl.when(p_owner)
@@ -219,9 +220,10 @@
         bulk(p_recv, ps_sem, pr_sem).wait_recv()
         p_all[p_mine] = p_own[p_mine] + jnp.sum(p_recv[...], axis=0)
         tile = p_all.at[p_mine]
-        for plane, gy, gx, gc in far_first((2.5, 1.5, 1, 0), 2):
-            z = (0, 3, 1, 2)[plane] * (3 - fz) + plane * (fz - 2)
-            remote(tile, tile, pbs_sem, pbr_sem, 2 * chip_at(z, gy, gx) + (1 - gc)).start()
+        for plane, gy, gx, gc in far_first((3, 2, 1, 0), 2):
+            z = (0, 1, 5 - fz, fz)[plane]
+            there = chip_at(z, gy, gx)
+            remote(tile, tile, pbs_sem, pbr_sem, 2 * there + flip(core, gc)).start()
 
     pl.loop(early, nc)(build)
 
@@ -249,7 +251,7 @@
     def pair(k):
         gy, gx = 1 - lax.div(k, 2), 1 - lax.rem(k, 2)
         column = 2 * (flip(fx, gx) + 2 * flip(fy, gy))
-        return [(lax.rem(fz + i, 2) + column, chip_at(1 + lax.rem(fz + i, 2), gy, gx)) for i in range(2)]
+        return [(lax.rem(fz + i, 2) + column, chip_at(lax.rem(fz + i, 2), gy, gx)) for i in range(2)]
 
     @pl.loop(0, n_half // 2)
     def _(k):
@@ -281,10 +283,19 @@
         bulk(y_recv, ys_sem, yr_sem).wait_recv()
         q_ref[q_mine] = (y_own[y_mine] + jnp.sum(y_recv[...], axis=0)) * (1.0 / n)
         tile = q_ref.at[q_mine]
-        for plane, gy, gx, _ in far_first((2, 1, 1, 0), 1):
-            there = (3, 0, 2, 1)[plane]
-            z = there * (2 - fz) + (3 - there) * (fz - 1)
-            remote(tile, tile, ybs_sem, ybr_sem.at[y_mine], 2 * chip_at(z, gy, gx) + core).start()
+
+        @pl.when(here != 0)
+        def _():
+            remote(tile, tile, ybs_sem, ybr_sem.at[y_mine], core).start()
+            remote(tile, tile, ybs_sem, qm_sem, 1 - core).start()
+
+        for plane, gy, gx, _ in far_first((2.5, 1.5, 1, 0), 1):
+            there = chip_at((3, 2, 1 - fz, fz)[plane], gy, gx)
+
+            @pl.when(there != 0)
+            def _():
+                remote(tile, tile, ybs_sem, ybr_sem.at[y_mine], 2 * there + core).start()
+
         remote(tile, tile, ybs_sem, qm_sem, mate).start()
 
     for s in range(n_half):
@@ -292,7 +303,10 @@
         def _():
             tile = q_ref.at[core * n_half + s]
             bulk(tile, ybs_sem, ybr_sem.at[s]).wait_recv()
-            remote(tile, tile, qs_sem, qm_sem, mate).start()
+
+            @pl.when(here != 0)
+            def _():
+                remote(tile, tile, qs_sem, qm_sem, mate).start()
 
     bulk(q_ref.at[pl.ds(0, n_half)], qs_sem, qm_sem).wait_recv()
     bulk(y_mate.at[pl.ds(0, n_half)], ms_sem, yr_sem).wait_send()
@@ -309,7 +323,14 @@
     @pl.when(y_owner)
     def _():
         bulk(y_own.at[pl.ds(0, n_half - 1)], ys_sem, yr_sem).wait_send()
+
+    @pl.when(here == 0)
+    def _():
         bulk(q_ref, ybs_sem, qm_sem).wait_send()
+
+    @pl.when(y_owner & (here != 0))
+    def _():
+        bulk(parts.at[0, pl.ds(0, (2 * n_half + 1) * RANK * cw // 64)], ybs_sem, qm_sem).wait_send()
         bulk(q_ref.at[pl.ds(0, n_half - 1)], qs_sem, qm_sem).wait_send()
 
     @pl.when(jnp.logical_not(y_owner))

time: 46.5 us -> 46.2 us (level)
  no operation moved by 1% of the time
where the time goes in v8:
time: 46.2 us; the launch traced here: 46 us
  Pallas kernels  45.4 us (98%)
  between operations  0.64 us (1%)
    pallas_call x1, Pallas kernels, per_device(): pl.pallas_call(functools.partial(reduce_kernel, n), out_shape=(pltpu.VMEM...  39.3 us
    pallas_call x1, Pallas kernels, per_device(): pl.pallas_call(apply_kernel, out_shape=(jax.ShapeDtypeStruct((RANK, d_in)...  6.14 us

profile of v8, /device:TPU:0, one launch (start us, length us, event | category | flops | bytes accessed | tf_op | source)
XLA Modules:
  0.0 46.0 jit_solution(2195313665423269749)
XLA Ops:
  0.6 39.3 %reduce_kernel.1 = (bf16[1024,128]{1,0:T(8,128)(2,1)S(1)}, f32[8,1024]{1,0:T(8,128)S(1)}, f32[16,8,256]{2,1,0:T(8,128)S(1)}, f32[1024,4096]{1,0:T(8,128)S(1)}) custom-call(bf16[512,1024]{1,0:T(8,128)(2,1)} %a_hbm.1, bf16[512,4096]{1,0:T(8,128)(2,1)} %z_hbm.1, bf16[512,4096]{1,0:T(8,128)(2,1)} %dy_hbm.1, f32[8,4096]{1,0:T(8,128)} %bitcast.3, ...), custom_call_target="tpu_custom_call" | custom-call | tf_op jit(solution)/shard_map/reduce_kernel/pallas_call | solution.py:387
  39.9 6.1 %apply_kernel.1 = (f32[8,1024]{1,0:T(8,128)}, f32[8,4096]{1,0:T(8,128)}, f32[1,1024,4096]{2,1,0:T(8,128)}) custom-call(bf16[1024,128]{1,0:T(8,128)(2,1)S(1)} %get-tuple-element.10.pleft_ref, f32[8,1024]{1,0:T(8,128)S(1)} %get-tuple-element.11.pt_ref, f32[16,8,256]{2,1,0:T(8,128)S(1)} %get-tuple-element.12.q_ref, f32[1024,4096]{1,0:T(8,128)S(1)} %get-tuple-element.13.m_ref), custom_call_target="tpu_custom_call" | custom-call | tf_op jit(solution)/shard_map/apply_kernel/pallas_call | solution.py:421

commit v9 on v2

--- a/solution.py
+++ b/solution.py
@@ -77,8 +77,8 @@
                   in_sem, q_sem, a_sem, ps_sem, pr_sem, pbs_sem, pbr_sem,
                   ms_sem, mr_sem, ys_sem, yr_sem, ybs_sem, ybr_sem):
     me = lax.axis_index("data")
-    d_in, d_out = m_ref.shape
-    tokens = z_v.shape[0]
+    d_in, tokens = at_v.shape
+    d_out = qt_v.shape[1]
     n_p = d_in // 128
     n_half = y_own.shape[0]
     cw = d_out // (2 * n_half)
@@ -94,17 +94,16 @@
 
     barrier = pltpu.get_barrier_semaphore()
 
-    def e_copy(c):
-        cols = pl.ds(pl.multiple_of(c * CB, CB), CB)
-        return pltpu.make_async_copy(e_hbm.at[0, :, cols], m_ref.at[:, cols], in_sem.at[c])
-
-    def z_copy(c):
-        cols = pl.ds(pl.multiple_of(c * CB, CB), CB)
-        return pltpu.make_async_copy(z_hbm.at[:, cols], z_v.at[:, cols], in_sem.at[c])
-
-    def dy_copy(c):
-        cols = pl.ds(pl.multiple_of(c * CB, CB), CB)
-        return pltpu.make_async_copy(dy_hbm.at[:, cols], dy_v.at[:, cols], in_sem.at[c])
+    def fetch(c):
+        for h in range(CB // 128):
+            i = c * (CB // 128) + h
+            cols = pl.ds(pl.multiple_of(i * 128, 128), 128)
+            pltpu.make_async_copy(z_hbm.at[:, cols], z_v.at[i], in_sem.at[c]).start()
+            pltpu.make_async_copy(dy_hbm.at[:, cols], dy_v.at[i], in_sem.at[c]).start()
+            pltpu.make_async_copy(e_hbm.at[0, :, cols], m_ref.at[i], in_sem.at[c]).start()
+
+    def wide(ref, c, rows):
+        return jnp.concatenate([ref[c * (CB // 128) + h, rows, :] for h in range(CB // 128)], axis=1)
 
     nc = d_out // CB
     q_copy = pltpu.make_async_copy(qt_hbm, qt_v, q_sem)
@@ -113,9 +112,7 @@
 
     @pl.loop(0, nc)
     def _(c):
-        z_copy(c).start()
-        dy_copy(c).start()
-        e_copy(c).start()
+        fetch(c)
 
         @pl.when(c == nc // 2)
         def _():
@@ -145,11 +142,11 @@
             qc = qs[:, cols]
             for r in range(d_in // RB):
                 rows = pl.ds(r * RB, RB)
-                e1, e2, e3 = split3(m_ref[rows, cols])
+                e1, e2, e3 = split3(wide(m_ref, c, rows))
                 p_acc[:, rows] += (mm_nt(qc, e3) + mm_nt(qc, e2)) + mm_nt(qc, e1)
                 if r % 2 == 1 and r // 2 < tokens // RB:
                     rows = pl.ds(r // 2 * RB, RB)
-                    gb = gelu_grad(z_v[rows, cols], dy_v[rows, cols]).astype(BF16)
+                    gb = gelu_grad(wide(z_v, c, rows), wide(dy_v, c, rows)).astype(BF16)
                     for h in range(CB // 128):
                         g[2 * c + h, rows, :] = gb[:, h * 128:(h + 1) * 128]
                     h_acc[:, rows] += mm_nt(qc, gb)
@@ -202,12 +199,12 @@
         at_v[rows, :] = a_v[:, rows].T
 
     def build(c):
-        cols = pl.ds(pl.multiple_of(c * CB, CB), CB)
-        gc = jnp.concatenate([g[2 * c + h] for h in range(CB // 128)], axis=1)
+        gc = wide(g, c, pl.ds(0, tokens))
         for r in range(d_in // RB):
             rows = pl.ds(r * RB, RB)
-            m = mm(at_v[rows, :], gc) * (1.0 / tokens) + m_ref[rows, cols]
-            m_ref[rows, cols] = m
+            m = mm(at_v[rows, :], gc) * (1.0 / tokens) + wide(m_ref, c, rows)
+            for h in range(CB // 128):
+                m_ref[2 * c + h, rows, :] = m[:, h * 128:(h + 1) * 128]
             for i, part in enumerate(split3(m)):
                 for h in range(CB // 128):
                     parts[2 * c + h, pl.ds(i * d_in + r * RB, RB), :] = part[:, h * 128:(h + 1) * 128]
@@ -304,7 +301,7 @@
 
 
 def apply_kernel(pleft_ref, pt_ref, q_ref, m_ref, p_out, q_out, e_out, stage, p_sem, q_sem, e_sem):
-    d_in, d_out = m_ref.shape
+    d_in = pleft_ref.shape[0]
     n_y, _, cw = q_ref.shape
     p_copy = pltpu.make_async_copy(pt_ref, p_out, p_sem)
     fill = jnp.zeros((128 - 9 * RANK, cw), F32)
@@ -324,7 +321,8 @@
         qc = jnp.concatenate(three * 3 + [fill], axis=0).astype(BF16)
         for r in range(d_in // RB):
             rows = pl.ds(r * RB, RB)
-            stage[rows, cols] = m_ref[rows, cols] - mm(pleft_ref[rows, :], qc)
+            m = jnp.concatenate([m_ref[c * (cw // 128) + h, rows, :] for h in range(cw // 128)], axis=1)
+            stage[rows, cols] = m - mm(pleft_ref[rows, :], qc)
         e_copy(c).start()
 
     p_copy.start()
@@ -354,15 +352,15 @@
                 pltpu.VMEM((d_in, 128), BF16),
                 pltpu.VMEM((RANK, d_in), F32),
                 pltpu.VMEM((n_y, RANK, cw), F32),
-                pltpu.VMEM((d_in, d_out), F32),
+                pltpu.VMEM((d_out // 128, d_in, 128), F32),
             ),
             in_specs=[hbm] * 5,
             out_specs=(vmem,) * 4,
             scratch_shapes=[
                 pltpu.VMEM((d_out // 128, 3 * d_in, 128), BF16),
                 pltpu.VMEM((d_out // 128, tokens, 128), BF16),
-                pltpu.VMEM((tokens, d_out), BF16),
-                pltpu.VMEM((tokens, d_out), BF16),
+                pltpu.VMEM((d_out // 128, tokens, 128), BF16),
+                pltpu.VMEM((d_out // 128, tokens, 128), BF16),
                 pltpu.VMEM((tokens, d_in), BF16),
                 pltpu.VMEM((d_in, tokens), BF16),
                 pltpu.VMEM((RANK, d_out), F32),

time: 45.9 us -> 46.1 us (level)
  no operation moved by 1% of the time
where the time goes in v9:
time: 46.1 us; the launch traced here: 45.9 us
  Pallas kernels  45.3 us (98%)
  between operations  0.64 us (1%)
    pallas_call x1, Pallas kernels, per_device(): pl.pallas_call(functools.partial(reduce_kernel, n), out_shape=(pltpu.VMEM...  39.2 us
    pallas_call x1, Pallas kernels, per_device(): pl.pallas_call(apply_kernel, out_shape=(jax.ShapeDtypeStruct((RANK, d_in)...  6.13 us

profile of v9, /device:TPU:0, one launch (start us, length us, event | category | flops | bytes accessed | tf_op | source)
XLA Modules:
  0.0 45.9 jit_solution(13670269622280731399)
XLA Ops:
  0.6 39.2 %reduce_kernel.1 = (bf16[1024,128]{1,0:T(8,128)(2,1)S(1)}, f32[8,1024]{1,0:T(8,128)S(1)}, f32[16,8,256]{2,1,0:T(8,128)S(1)}, f32[32,1024,128]{2,1,0:T(8,128)S(1)}) custom-call(bf16[512,1024]{1,0:T(8,128)(2,1)} %a_hbm.1, bf16[512,4096]{1,0:T(8,128)(2,1)} %z_hbm.1, bf16[512,4096]{1,0:T(8,128)(2,1)} %dy_hbm.1, f32[8,4096]{1,0:T(8,128)} %bitcast.3, ...), custom_call_target="tpu_custom_call" | custom-call | tf_op jit(solution)/shard_map/reduce_kernel/pallas_call | solution.py:349
  39.8 6.1 %apply_kernel.1 = (f32[8,1024]{1,0:T(8,128)}, f32[8,4096]{1,0:T(8,128)}, f32[1,1024,4096]{2,1,0:T(8,128)}) custom-call(bf16[1024,128]{1,0:T(8,128)(2,1)S(1)} %get-tuple-element.10.pleft_ref, f32[8,1024]{1,0:T(8,128)S(1)} %get-tuple-element.11.pt_ref, f32[16,8,256]{2,1,0:T(8,128)S(1)} %get-tuple-element.12.q_ref, f32[32,1024,128]{2,1,0:T(8,128)S(1)} %get-tuple-element.13.m_ref), custom_call_target="tpu_custom_call" | custom-call | tf_op jit(solution)/shard_map/apply_kernel/pallas_call | solution.py:383

commit v10 on v2

--- a/solution.py
+++ b/solution.py
@@ -177,14 +177,20 @@
     def bulk(ref, send_sem, recv_sem):
         return remote(ref, ref, send_sem, recv_sem, me)
 
-    def broadcast(buf, index, send_sem, recv_sem):
+    def broadcast(buf, index, send_sem, recv_sem, first=0):
+        for there in range(first):
+            remote(buf.at[index], buf.at[index], send_sem, recv_sem, there).start()
         for plane, gy, gx, gc in far_first():
             there = (3, 0, 2, 1)[plane]
             z = there * (2 - fz) + (3 - there) * (fz - 1)
             y = 1 - fy if gy else fy
             x = 1 - fx if gx else fx
             c = 1 - core if gc else core
-            remote(buf.at[index], buf.at[index], send_sem, recv_sem, z * 8 + y * 4 + x * 2 + c).start()
+            there = z * 8 + y * 4 + x * 2 + c
+
+            @pl.when(there >= first)
+            def _():
+                remote(buf.at[index], buf.at[index], send_sem, recv_sem, there).start()
 
     p_owner = central & (core == 1)
 
@@ -278,7 +284,7 @@
     def _():
         bulk(y_recv, ys_sem, yr_sem).wait_recv()
         q_ref[q_mine] = (y_own[mine] + jnp.sum(y_recv[...], axis=0)) * (1.0 / n)
-        broadcast(q_ref, q_mine, ybs_sem, ybr_sem)
+        broadcast(q_ref, q_mine, ybs_sem, ybr_sem, first=2)
 
     bulk(y_mate.at[pl.ds(0, n_half)], ms_sem, yr_sem).wait_send()
 

time: 45.9 us -> 45.6 us (level)
  no operation moved by 1% of the time
where the time goes in v10:
time: 45.6 us; the launch traced here: 45.3 us
  Pallas kernels  44.7 us (98%)
  between operations  0.64 us (1%)
    pallas_call x1, Pallas kernels, per_device(): pl.pallas_call(functools.partial(reduce_kernel, n), out_shape=(pltpu.VMEM...  38.5 us
    pallas_call x1, Pallas kernels, per_device(): pl.pallas_call(apply_kernel, out_shape=(jax.ShapeDtypeStruct((RANK, d_in)...  6.13 us

profile of v10, /device:TPU:0, one launch (start us, length us, event | category | flops | bytes accessed | tf_op | source)
XLA Modules:
  0.0 45.3 jit_solution(10895916705408610673)
XLA Ops:
  0.6 38.5 %reduce_kernel.1 = (bf16[1024,128]{1,0:T(8,128)(2,1)S(1)}, f32[8,1024]{1,0:T(8,128)S(1)}, f32[16,8,256]{2,1,0:T(8,128)S(1)}, f32[1024,4096]{1,0:T(8,128)S(1)}) custom-call(bf16[512,1024]{1,0:T(8,128)(2,1)} %a_hbm.1, bf16[512,4096]{1,0:T(8,128)(2,1)} %z_hbm.1, bf16[512,4096]{1,0:T(8,128)(2,1)} %dy_hbm.1, f32[8,4096]{1,0:T(8,128)} %bitcast.3, ...), custom_call_target="tpu_custom_call" | custom-call | tf_op jit(solution)/shard_map/reduce_kernel/pallas_call | solution.py:357
  39.2 6.1 %apply_kernel.1 = (f32[8,1024]{1,0:T(8,128)}, f32[8,4096]{1,0:T(8,128)}, f32[1,1024,4096]{2,1,0:T(8,128)}) custom-call(bf16[1024,128]{1,0:T(8,128)(2,1)S(1)} %get-tuple-element.10.pleft_ref, f32[8,1024]{1,0:T(8,128)S(1)} %get-tuple-element.11.pt_ref, f32[16,8,256]{2,1,0:T(8,128)S(1)} %get-tuple-element.12.q_ref, f32[1024,4096]{1,0:T(8,128)S(1)} %get-tuple-element.13.m_ref), custom_call_target="tpu_custom_call" | custom-call | tf_op jit(solution)/shard_map/apply_kernel/pallas_call | solution.py:391

commit v11 on v10

--- a/solution.py
+++ b/solution.py
@@ -92,6 +92,11 @@
     def owner_chip(s):
         return 4 * (1 + lax.rem(s, 2)) + lax.div(s, 2)
 
+    y_mine = jnp.minimum(jnp.maximum(2 - fz, 0), 1) + 2 * (3 - fx - 2 * fy)
+
+    def y_chip(s):
+        return 4 * (2 - lax.rem(s, 2)) + 3 - lax.div(s, 2)
+
     barrier = pltpu.get_barrier_semaphore()
 
     def e_copy(c):
@@ -268,7 +273,7 @@
             y_own[s] = y_tile(core * n_half + s) + y_mate[n_half + s]
         for i in range(2):
             s = 2 * k + i
-            chip = owner_chip(s)
+            chip = y_chip(s)
             slot = lax.rem(lax.div(me, 2) - chip + n - 1, n // 2)
 
             @pl.when(me != 2 * chip + core)
@@ -278,12 +283,12 @@
     p1, p2, p3 = [x.astype(F32) for x in split3(p)]
     fill = jnp.zeros((128 - 9 * RANK, d_in), F32)
     pleft_ref[...] = jnp.concatenate([p1] * 3 + [p2] * 3 + [p3] * 3 + [fill], axis=0).T.astype(BF16)
-    q_mine = core * n_half + mine
+    q_mine = core * n_half + y_mine
 
     @pl.when(central)
     def _():
         bulk(y_recv, ys_sem, yr_sem).wait_recv()
-        q_ref[q_mine] = (y_own[mine] + jnp.sum(y_recv[...], axis=0)) * (1.0 / n)
+        q_ref[q_mine] = (y_own[y_mine] + jnp.sum(y_recv[...], axis=0)) * (1.0 / n)
         broadcast(q_ref, q_mine, ybs_sem, ybr_sem, first=2)
 
     bulk(y_mate.at[pl.ds(0, n_half)], ms_sem, yr_sem).wait_send()

time: 45.6 us -> 45.8 us (level)
  no operation moved by 1% of the time
where the time goes in v11:
time: 45.8 us; the launch traced here: 45.7 us
  Pallas kernels  45 us (98%)
  between operations  0.64 us (1%)
    pallas_call x1, Pallas kernels, per_device(): pl.pallas_call(functools.partial(reduce_kernel, n), out_shape=(pltpu.VMEM...  38.9 us
    pallas_call x1, Pallas kernels, per_device(): pl.pallas_call(apply_kernel, out_shape=(jax.ShapeDtypeStruct((RANK, d_in)...  6.13 us

profile of v11, /device:TPU:0, one launch (start us, length us, event | category | flops | bytes accessed | tf_op | source)
XLA Modules:
  0.0 45.7 jit_solution(14469934537374125822)
XLA Ops:
  0.6 38.9 %reduce_kernel.1 = (bf16[1024,128]{1,0:T(8,128)(2,1)S(1)}, f32[8,1024]{1,0:T(8,128)S(1)}, f32[16,8,256]{2,1,0:T(8,128)S(1)}, f32[1024,4096]{1,0:T(8,128)S(1)}) custom-call(bf16[512,1024]{1,0:T(8,128)(2,1)} %a_hbm.1, bf16[512,4096]{1,0:T(8,128)(2,1)} %z_hbm.1, bf16[512,4096]{1,0:T(8,128)(2,1)} %dy_hbm.1, f32[8,4096]{1,0:T(8,128)} %bitcast.3, ...), custom_call_target="tpu_custom_call" | custom-call | tf_op jit(solution)/shard_map/reduce_kernel/pallas_call | solution.py:362
  39.5 6.1 %apply_kernel.1 = (f32[8,1024]{1,0:T(8,128)}, f32[8,4096]{1,0:T(8,128)}, f32[1,1024,4096]{2,1,0:T(8,128)}) custom-call(bf16[1024,128]{1,0:T(8,128)(2,1)S(1)} %get-tuple-element.10.pleft_ref, f32[8,1024]{1,0:T(8,128)S(1)} %get-tuple-element.11.pt_ref, f32[16,8,256]{2,1,0:T(8,128)S(1)} %get-tuple-element.12.q_ref, f32[1024,4096]{1,0:T(8,128)S(1)} %get-tuple-element.13.m_ref), custom_call_target="tpu_custom_call" | custom-call | tf_op jit(solution)/shard_map/apply_kernel/pallas_call | solution.py:396

commit v12 on v10

--- a/solution.py
+++ b/solution.py
@@ -65,10 +65,10 @@
     return w / jnp.sqrt(norm2)
 
 
-def far_first():
+def far_first(planes):
     places = [(i, fy, fx, fc) for i in range(4) for fy in range(2) for fx in range(2) for fc in range(2)]
     places.remove((3, 0, 0, 0))
-    return sorted(places, key=lambda p: -((2, 1, 1, 0)[p[0]] + p[1] + p[2]))
+    return sorted(places, key=lambda p: -(planes[p[0]] + p[1] + p[2]))
 
 
 def reduce_kernel(n, a_hbm, z_hbm, dy_hbm, qt_hbm, e_hbm, pleft_ref, pt_ref, q_ref, m_ref,
@@ -180,7 +180,7 @@
     def broadcast(buf, index, send_sem, recv_sem, first=0):
         for there in range(first):
             remote(buf.at[index], buf.at[index], send_sem, recv_sem, there).start()
-        for plane, gy, gx, gc in far_first():
+        for plane, gy, gx, gc in far_first((2, 1, 1, 0)):
             there = (3, 0, 2, 1)[plane]
             z = there * (2 - fz) + (3 - there) * (fz - 1)
             y = 1 - fy if gy else fy
@@ -192,11 +192,16 @@
             def _():
                 remote(buf.at[index], buf.at[index], send_sem, recv_sem, there).start()
 
-    p_owner = central & (core == 1)
+    here = lax.div(me, 2)
+    last = n // 2 - 1
+    p_owner = (here >= last - 2) | (here == last - 4)
+    p_mine = 2 * jnp.minimum(last - here, n_p // 2 - 1) + core
 
     @pl.loop(0, n_p)
-    def _(b):
-        owner = 2 * owner_chip(b) + 1
+    def _(k):
+        b = lax.rem(k + me, n_p)
+        near = lax.div(b, 2)
+        owner = 2 * (last - near - lax.div(near, 3)) + lax.rem(b, 2)
 
         @pl.when(me != owner)
         def _():
@@ -218,15 +223,22 @@
                 for h in range(CB // 128):
                     parts[2 * c + h, pl.ds(i * d_in + r * RB, RB), :] = part[:, h * 128:(h + 1) * 128]
 
-    pl.loop(0, nc // 2 + 1)(build)
+    early = jnp.where(here == last, 3, 6)
+    pl.loop(0, early)(build)
 
     @pl.when(p_owner)
     def _():
         bulk(p_recv, ps_sem, pr_sem).wait_recv()
-        p_all[mine] = p_own[mine] + jnp.sum(p_recv[...], axis=0)
-        broadcast(p_all, mine, pbs_sem, pbr_sem)
-
-    pl.loop(nc // 2 + 1, nc)(build)
+        p_all[p_mine] = p_own[p_mine] + jnp.sum(p_recv[...], axis=0)
+        tile = p_all.at[p_mine]
+        for plane, gy, gx, gc in far_first((3, 2, 1, 0)):
+            z = (0, 1, 5 - fz, fz)[plane]
+            y = 1 - fy if gy else fy
+            x = 1 - fx if gx else fx
+            c = 1 - core if gc else core
+            remote(tile, tile, pbs_sem, pbr_sem, z * 8 + y * 4 + x * 2 + c).start()
+
+    pl.loop(early, nc)(build)
 
     @pl.when(p_owner)
     def _():

time: 45.6 us -> 46.4 us (1.018)
  Pallas kernels: 44.7 us -> 45.3 us
    pallas_call x1, Pallas kernels: 38.5 us -> 39.2 us  [per_device(): pl.pallas_call(functools.partial(reduce_kernel, n), out_shape=(pltpu.VMEM...]
where the time goes in v12:
time: 46.4 us; the launch traced here: 46 us
  Pallas kernels  45.3 us (98%)
  between operations  0.64 us (1%)
    pallas_call x1, Pallas kernels, per_device(): pl.pallas_call(functools.partial(reduce_kernel, n), out_shape=(pltpu.VMEM...  39.2 us
    pallas_call x1, Pallas kernels, per_device(): pl.pallas_call(apply_kernel, out_shape=(jax.ShapeDtypeStruct((RANK, d_in)...  6.14 us

profile of v12, /device:TPU:0, one launch (start us, length us, event | category | flops | bytes accessed | tf_op | source)
XLA Modules:
  0.0 46.0 jit_solution(1999445639627688709)
XLA Ops:
  0.6 39.2 %reduce_kernel.1 = (bf16[1024,128]{1,0:T(8,128)(2,1)S(1)}, f32[8,1024]{1,0:T(8,128)S(1)}, f32[16,8,256]{2,1,0:T(8,128)S(1)}, f32[1024,4096]{1,0:T(8,128)S(1)}) custom-call(bf16[512,1024]{1,0:T(8,128)(2,1)} %a_hbm.1, bf16[512,4096]{1,0:T(8,128)(2,1)} %z_hbm.1, bf16[512,4096]{1,0:T(8,128)(2,1)} %dy_hbm.1, f32[8,4096]{1,0:T(8,128)} %bitcast.3, ...), custom_call_target="tpu_custom_call" | custom-call | tf_op jit(solution)/shard_map/reduce_kernel/pallas_call | solution.py:369
  39.8 6.1 %apply_kernel.1 = (f32[8,1024]{1,0:T(8,128)}, f32[8,4096]{1,0:T(8,128)}, f32[1,1024,4096]{2,1,0:T(8,128)}) custom-call(bf16[1024,128]{1,0:T(8,128)(2,1)S(1)} %get-tuple-element.10.pleft_ref, f32[8,1024]{1,0:T(8,128)S(1)} %get-tuple-element.11.pt_ref, f32[16,8,256]{2,1,0:T(8,128)S(1)} %get-tuple-element.12.q_ref, f32[1024,4096]{1,0:T(8,128)S(1)} %get-tuple-element.13.m_ref), custom_call_target="tpu_custom_call" | custom-call | tf_op jit(solution)/shard_map/apply_kernel/pallas_call | solution.py:403
